TPU v7x, 256 devices: a 8x8x2 block of a 8x8x16 slice. The times are simulated.
256 devices in a mesh: groups: 2 (over z), seq: 64 (over y, x), expert: 2 (over core).
Axes of the slice: x: 8, y: 8, z: 2, core: 2. Of those that a mesh axis runs over, the one named last changes fastest.
The devices are a block of a 8x8x16 slice.
Arguments:
- residual: bfloat16 [8, 6144], P('groups', 'seq'), parts along dimension 0, may hold values from -27 to 27
- queries: bfloat16 [8, 6144], P('groups', 'expert'), parts along dimension 0, may hold values from -6 to 6
- new_entries: bfloat16 [2, 8, 1024], P(None, 'groups', 'expert'), parts along dimension 1, may hold values from -6 to 6
- kv_cache: bfloat16 [2, 1024, 131072], P(None, 'seq', ('groups', 'expert')), parts along dimension 2, may hold values from -6 to 6
- lengths: int32 [8], P('groups'), parts along dimension 0, may hold values from 1024 to 16384, as said below
- routing: int32 [8, 2], P('groups'), parts along dimension 0, may hold values from 0 to 3, all different within a row
- w_out: bfloat16 [6144, 6144], P('expert', 'seq'), may hold values from -0.5 to 0.5
- norm_gain: bfloat16 [6144], replicated, may hold values from 0.5 to 1.5
- router: bfloat16 [6144, 4], replicated, may hold values from -0.078125 to 0.078125
- w_gate: bfloat16 [4, 6144, 8192], P('expert', None, 'seq'), may hold values from -0.078125 to 0.078125
- w_up: bfloat16 [4, 6144, 8192], P('expert', None, 'seq'), may hold values from -0.078125 to 0.078125
- w_down: bfloat16 [4, 8192, 6144], P('expert', 'seq'), may hold values from -0.5 to 0.5
Outputs:
- attended: bfloat16 [8, 6144], P('groups', 'seq'), parts along dimension 0
- expert_out: bfloat16 [8, 6144], P('groups', 'seq'), parts along dimension 0
There are 2 independent parts, one for each index of `groups`. A program takes and returns all parts, laid end to end along the dimension named above; an argument that names none is the same for every part. Nothing has to cross between parts.
Inputs may be any that keep to these rules, and one draw needn't show every extreme that they name: `lengths`: every draw has a request of exactly 16384 positions. `routing`: each request names two different experts.
All inputs are finite; a program needn't handle non-finite values.
Results may differ from a plain program's by a relative error of at most 0.02.
Values may be sent and summed in bfloat16 or wider, within the bound.
No kernel may reach another device: no remote copies, remote signals or barrier semaphores. Data moves between devices by JAX's collectives and lax.ppermute only.
A program may use at most 128 MiB of HBM per device.

v0:
```python
import math

import jax
import jax.numpy as jnp
from jax import lax
from jax.sharding import Mesh
from jax.sharding import PartitionSpec as P

H = 48
KVH = 8
HD = 128
SEQ = ("seq_0", "seq_1")
SEQ_EXPERT = ("seq_0", "seq_1", "expert")


def from_everyone(shard, axis):
    copies = jnp.broadcast_to(shard, (lax.axis_size(axis), *shard.shape))
    return lax.all_to_all(copies, axis, split_axis=0, concat_axis=0, tiled=True)


def in_order(parts, dim):
    parts = jnp.moveaxis(parts, 0, dim)
    lengths = parts.shape
    return parts.reshape(*lengths[:dim], lengths[dim] * lengths[dim + 1], *lengths[dim + 2 :])


def collect(shard, axis, dim):
    parts = from_everyone(shard, axis)
    return in_order(parts, dim)


def collected_together(shard, axis):
    leaves = jax.tree.leaves(shard)
    turns = sorted(range(len(leaves)), key=lambda k: -leaves[k].size)
    width = (1, *leaves[turns[0]].shape)[-1]
    lines = [
        jnp.pad(leaves[k].reshape(-1), (0, -leaves[k].size % width)).reshape(-1, width)
        for k in turns
    ]
    both, at, found = (lax.all_gather(jnp.concatenate(lines), axis), 0, {})
    for k, line in zip(turns, lines):
        share = both[:, at : at + len(line)].reshape(len(both), -1)
        found[k] = share[:, : leaves[k].size].reshape(-1, *leaves[k].shape)
        at += len(line)
    numbers = iter(range(len(leaves)))
    return jax.tree.map(lambda _: found[next(numbers)], shard)


def merged_by_axis(shard, axes, combine):
    for axis in axes:
        pieces = collected_together(shard, axis)
        shard = jax.tree.map(lambda part: part[0], pieces)
        for k in range(1, lax.axis_size(axis)):
            shard = combine(shard, jax.tree.map(lambda part: part[k], pieces))
    return shard


def over_pieces(shard, axis):
    parts = lax.all_gather(shard, axis)
    return parts.sum(axis=0)


def in_blocks(shard, dim, peers):
    lengths = shard.shape
    parts = shard.reshape(*lengths[:dim], peers, lengths[dim] // peers, *lengths[dim + 1 :])
    return jnp.moveaxis(parts, dim, 0)


def sum_at_owner(shard, axis, dim):
    parts = in_blocks(shard, dim, lax.axis_size(axis))
    arrived = lax.all_to_all(parts, axis, split_axis=0, concat_axis=0, tiled=True)
    return arrived.sum(axis=0)


def merge_parts(earlier, later):
    high_left, total_left, sum_left = earlier
    high_right, total_right, sum_right = later
    joined = jnp.maximum(high_left, high_right)
    scale_left = jnp.exp(high_left - joined)
    scale_right = jnp.exp(high_right - joined)
    return (
        joined,
        total_left * scale_left + total_right * scale_right,
        sum_left * scale_left[..., None] + sum_right * scale_right[..., None],
    )


def partial_attention(query_rows, relaid, positions, lengths, kv_count):
    requests = lengths.shape[0]
    per_group = H // KVH
    slot_count = relaid.shape[2] // requests
    query_heads = query_rows.reshape(requests, kv_count, per_group, HD)
    key_rows = relaid[0].reshape(kv_count, HD, slot_count, requests)
    value_rows = relaid[1].reshape(kv_count, HD, slot_count, requests)
    scores = jnp.einsum(
        "rgtd,gdpr->rgtp", query_heads, key_rows, preferred_element_type=jnp.float32
    ) * (1.0 / math.sqrt(HD))
    alive_mask = (positions[None, :] < lengths[:, None])[:, None, None, :]
    highest = jnp.max(jnp.where(alive_mask, scores, -1e30), axis=-1)
    weights = jnp.where(alive_mask, jnp.exp(scores - highest[..., None]), 0.0)
    summed = jnp.einsum(
        "rgtp,gdpr->rgtd",
        weights.astype(jnp.bfloat16),
        value_rows,
        preferred_element_type=jnp.float32,
    )
    return (highest, jnp.sum(weights, axis=-1), summed)


def on_device(
    residual,
    queries,
    new_entries,
    kv_cache,
    lengths,
    routing,
    w_out,
    norm_gain,
    router,
    w_gate,
    w_up,
    w_down,
):
    requests = lengths.shape[0]
    seq_count = lax.axis_size(SEQ)
    core_count = lax.axis_size("expert")
    seq_index = lax.axis_index(SEQ)
    core_index = lax.axis_index("expert")
    half_ctx = kv_cache.shape[2] // requests
    ctx_dev = half_ctx // seq_count
    own_heads = KVH // core_count
    relaid = lax.all_to_all(kv_cache, SEQ, split_axis=2, concat_axis=1, tiled=True)
    positions = core_index * half_ctx + seq_index * ctx_dev + jnp.arange(ctx_dev, dtype=jnp.int32)
    all_queries = collect(queries, "expert", 1)
    partials = partial_attention(all_queries, relaid, positions, lengths, KVH)
    merged = merged_by_axis(partials, SEQ_EXPERT, merge_parts)
    head_start = core_index * own_heads
    highest = lax.dynamic_slice_in_dim(merged[0], head_start, own_heads, 1)
    totals = lax.dynamic_slice_in_dim(merged[1], head_start, own_heads, 1)
    summed = lax.dynamic_slice_in_dim(merged[2], head_start, own_heads, 1)
    per_group = H // KVH
    query_heads = queries.reshape(requests, own_heads, per_group, HD)
    new_keys = new_entries[0].reshape(requests, own_heads, HD)
    new_values = new_entries[1].reshape(requests, own_heads, HD).astype(jnp.float32)
    own_score = jnp.einsum(
        "rgtd,rgd->rgt", query_heads, new_keys, preferred_element_type=jnp.float32
    ) * (1.0 / math.sqrt(HD))
    joined = jnp.maximum(highest, own_score)
    fade_old = jnp.exp(highest - joined)
    own_weight = jnp.exp(own_score - joined)
    numerator = summed * fade_old[..., None] + own_weight[..., None] * new_values[:, :, None, :]
    denominator = totals * fade_old + own_weight
    attn_rows = (
        (numerator / denominator[..., None])
        .reshape(requests, own_heads * per_group * HD)
        .astype(jnp.bfloat16)
    )
    head_terms = jnp.dot(attn_rows, w_out, preferred_element_type=jnp.float32)
    attended = (residual.astype(jnp.float32) + over_pieces(head_terms, "expert")).astype(
        jnp.bfloat16
    )
    gathered = collect(attended, SEQ, 1)
    widened = gathered.astype(jnp.float32)
    mean_square = jnp.mean(widened * widened, axis=-1, keepdims=True)
    normed = (widened * lax.rsqrt(mean_square + 1e-05) * norm_gain.astype(jnp.float32)).astype(
        jnp.bfloat16
    )
    logits = jnp.dot(normed, router, preferred_element_type=jnp.float32)
    expert_total = router.shape[1]
    picked = (
        routing[:, :, None] == jnp.arange(expert_total, dtype=jnp.int32)[None, None, :]
    ).astype(jnp.float32)
    chosen = jnp.sum(picked * logits[:, None, :], axis=-1)
    first_share = jax.nn.sigmoid(chosen[:, 0] - chosen[:, 1])
    shares = jnp.stack([first_share, 1.0 - first_share], axis=-1)
    combine = jnp.sum(picked * shares[:, :, None], axis=1)
    local_ids = core_index * w_gate.shape[0] + jnp.arange(w_gate.shape[0], dtype=jnp.int32)
    select = (jnp.arange(expert_total, dtype=jnp.int32)[:, None] == local_ids[None, :]).astype(
        jnp.float32
    )
    local_share = jnp.sum(combine[:, :, None] * select[None, :, :], axis=1)
    gate_proj = jnp.einsum("rd,edf->ref", normed, w_gate, preferred_element_type=jnp.float32)
    upward = jnp.einsum("rd,edf->ref", normed, w_up, preferred_element_type=jnp.float32)
    activation = (jax.nn.silu(gate_proj) * upward * local_share[:, :, None]).astype(jnp.bfloat16)
    expert_terms = jnp.einsum("ref,efd->rd", activation, w_down, preferred_element_type=jnp.float32)
    reduced = sum_at_owner(expert_terms, SEQ, 1)
    expert_out = over_pieces(reduced, "expert").astype(jnp.bfloat16)
    return (attended, expert_out)


def solution(mesh):
    split = Mesh(
        mesh.devices.reshape(mesh.shape["groups"], 8, 8, mesh.shape["expert"]),
        ("groups", "seq_0", "seq_1", "expert"),
    )
    return jax.shard_map(
        on_device,
        mesh=split,
        in_specs=(
            P("groups", SEQ),
            P("groups", "expert"),
            P(None, "groups", "expert"),
            P(None, SEQ, ("groups", "expert")),
            P("groups"),
            P("groups", None),
            P("expert", SEQ),
            P(),
            P(),
            P("expert", None, SEQ),
            P("expert", None, SEQ),
            P("expert", SEQ, None),
        ),
        out_specs=(P("groups", SEQ), P("groups", SEQ)),
        check_vma=False,
    )
```

profile of v0, /device:TPU:513, one launch (start us, length us, event | category | flops | bytes accessed | tf_op | source)
XLA Modules:
  0.0 314.1 jit_solution(13413196184631363552)
XLA Ops:
  0.6 1.5 broadcast_in_dim.23
  2.2 23.7 %all-to-all-start = ((bf16[2,4,3072]{2,1,0:T(4,128)(2,1)}), bf16[2,4,3072]{2,1,0:T(4,128)(2,1)S(1)}, u32[]{:S(2)}, u32[]{:S(2)}) async-start(bf16[2,4,3072]{2,1,0:T(4,128)(2,1)} %broadcast_in_dim.23), calls=%async_computation | async-start | bytes 98304 | tf_op jit(solution)/shard_map/all_to_all | solution.py:18
  25.9 30.9 %copy.35 = bf16[2,16,32768]{1,0,2:T(2,128)(2,1)} copy(bf16[2,16,32768]{2,1,0:T(8,128)(2,1)} %param.15) | data formatting | bytes 4194304 | tf_op args[3]
  56.8 20.7 %reshape.1033 = bf16[64,2,8192]{2,1,0:T(2,128)(2,1)} reshape(bf16[32768,2,16]{2,1,0:T(2,128)(2,1)} %bitcast.267) | data formatting | bytes 4194304
  77.5 7.3 %all-to-all-start.1 = ((bf16[64,2,8192]{2,1,0:T(2,128)(2,1)}), bf16[64,2,8192]{2,1,0:T(2,128)(2,1)}, u32[]{:S(2)}, u32[]{:S(2)}) async-start(bf16[64,2,8192]{2,1,0:T(2,128)(2,1)} %reshape.1033), calls=%async_computation.1 | async-start | bytes 4194304 | tf_op jit(solution)/shard_map/all_to_all | solution.py:132
  85.0 0.6 reshape.983
  85.6 0.5 iota_add_fusion
  86.2 0.7 fusion.85
  86.9 48.9 %all-to-all-done.1 = bf16[64,2,8192]{2,1,0:T(2,128)(2,1)} async-done(((bf16[64,2,8192]{2,1,0:T(2,128)(2,1)}), bf16[64,2,8192]{2,1,0:T(2,128)(2,1)}, u32[]{:S(2)}, u32[]{:S(2)}) %all-to-all-start.1) | async-done | bytes 2097184 | tf_op jit(solution)/shard_map/all_to_all | solution.py:132
  135.9 16.5 %reshape.1034 = bf16[32768,2,16]{2,1,0:T(2,128)(2,1)} reshape(bf16[64,2,8192]{2,1,0:T(2,128)(2,1)} %all-to-all-done.1) | data formatting | bytes 4194304
  152.4 14.7 %copy.63 = bf16[2,16,64,512]{1,2,3,0:T(8,128)(2,1)S(1)} copy(bf16[2,16,64,512]{1,0,3,2:T(2,128)(2,1)} %bitcast.269) | data formatting | bytes 4194304 | tf_op jit(solution)/shard_map/all_to_all | solution.py:132
  167.2 7.3 %fusion.79 = (bf16[1,64,16,512]{2,1,3,0:T(8,128)(2,1)}, bf16[1,64,16,512]{2,1,3,0:T(8,128)(2,1)}) fusion(bf16[2,64,16,512]{2,1,3,0:T(8,128)(2,1)S(1)} %bitcast.268), kind=kLoop, calls=%fused_computation.182 | loop fusion | bytes 4194304 | tf_op jit(solution)/shard_map/slice | solution.py:94
  174.5 10.1 %reshape_squeeze.10 = bf16[8,128,128,4]{1,0,3,2:T(8,128)(2,1)} reshape(bf16[1,64,16,512]{2,1,3,0:T(8,128)(2,1)} %get-tuple-element.58) | data formatting | bytes 2097152 | tf_op jit(solution)/shard_map/reshape;squeeze | solution.py:93
  184.6 2.0 select_reduce_fusion
  186.5 0.1 reshape.967
  186.6 0.2 fusion.6
  186.8 0.1 reshape.969
  186.9 10.1 %reshape_squeeze.11 = bf16[8,128,128,4]{1,0,3,2:T(8,128)(2,1)} reshape(bf16[1,64,16,512]{2,1,3,0:T(8,128)(2,1)} %get-tuple-element.57) | data formatting | bytes 2097152 | tf_op jit(solution)/shard_map/reshape;squeeze | solution.py:94
  197.1 1.7 fusion.2
  198.8 21.3 %all-gather.5 = f32[8,196,128]{2,1,0:T(8,128)S(1)} all-gather(f32[1,196,128]{2,1,0:T(8,128)S(1)} %maximum_bitcast_fusion), channel_id=2, replica_groups=mesh['groups'=2,'seq_0'=8,'seq_1'=8,'expert'=2] {'seq_0'}, dimensions={0}, use_global_device_ids=true | all-gather | bytes 903168 | tf_op jit(solution)/shard_map/all_gather | solution.py:40
  220.2 0.4 fusion.30
  220.7 22.9 %all-gather.6 = f32[8,196,128]{2,1,0:T(8,128)S(1)} all-gather(f32[1,196,128]{2,1,0:T(8,128)S(1)} %maximum_bitcast_fusion.1), channel_id=3, replica_groups=mesh['groups'=2,'seq_0'=8,'seq_1'=8,'expert'=2] {'seq_1'}, dimensions={0}, use_global_device_ids=true | all-gather | bytes 903168 | tf_op jit(solution)/shard_map/all_gather | solution.py:40
  243.8 0.4 fusion.9
  244.2 12.4 %all-gather.7 = f32[2,196,128]{2,1,0:T(8,128)S(1)} all-gather(f32[1,196,128]{2,1,0:T(8,128)S(1)} %maximum_bitcast_fusion.2), channel_id=4, replica_groups=mesh['groups'=2,'seq_0'=8,'seq_1'=8,'expert'=2] {'expert'}, dimensions={0}, use_global_device_ids=true | all-gather | bytes 301056 | tf_op jit(solution)/shard_map/all_gather | solution.py:40
  256.8 0.1 squeeze.214
  257.1 0.1 squeeze.217
  257.2 0.7 squeeze.215
  257.9 0.7 fusion.67
  258.6 1.0 fusion.57
  259.6 1.3 convolution_bitcast_fusion.1
  260.9 1.9 all-gather.8
  262.8 0.7 add_convert_fusion
  263.5 0.6 broadcast_in_dim.26
  264.2 9.6 %all-to-all-start.2 = ((bf16[64,4,96]{2,1,0:T(4,128)(2,1)}), bf16[64,4,96]{2,1,0:T(4,128)(2,1)S(1)}, u32[]{:S(2)}, u32[]{:S(2)}) async-start(bf16[64,4,96]{2,1,0:T(4,128)(2,1)} %broadcast_in_dim.26), calls=%async_computation.2 | async-start | bytes 131072 | tf_op jit(solution)/shard_map/all_to_all | solution.py:18
  273.8 0.7 compare_convert_fusion
  274.5 0.7 convert_element_type.76
  275.2 8.4 %all-to-all-done.2 = bf16[64,4,96]{2,1,0:T(4,128)(2,1)S(1)} async-done(((bf16[64,4,96]{2,1,0:T(4,128)(2,1)}), bf16[64,4,96]{2,1,0:T(4,128)(2,1)S(1)}, u32[]{:S(2)}, u32[]{:S(2)}) %all-to-all-start.2) | async-done | bytes 49184 | tf_op jit(solution)/shard_map/all_to_all | solution.py:18
  283.7 0.1 reshape.984
  283.8 0.2 fusion.5
  284.1 1.0 fusion.86
  285.1 0.8 select_reduce_fusion.2
  286.0 0.8 select_reduce_fusion.1
  286.7 2.4 fusion.61
  289.2 3.7 %convolution_bitcast_fusion = f32[4,6144]{1,0:T(4,128)S(1)} fusion(bf16[2,128,6144]{2,1,0:T(8,128)(2,1)S(1)} %copy-done, bf16[2,6144,128]{2,1,0:T(8,128)(2,1)} %param.22, bf16[4,6144]{1,0:T(4,128)(2,1)S(1)} %multiply_convert_fusion, f32[4,2,128]{2,0,1:T(4,128)S(1)} %fusion.61, f32[4,2]{0,1:T(2,128)S(1)} %multiply_reduce_fusion), kind=kOutput, calls=%fused_computation.1 | convolution fusion | flops 25172992 | bytes 6443040 | tf_op jit(solution)/shard_map/ref,efd->rd/dot_general | solution.py:185
  292.9 0.1 reshape.982
  293.2 15.8 %all_to_all.30 = f32[64,4,96]{2,1,0:T(4,128)S(1)} all-to-all(f32[64,4,96]{2,1,0:T(4,128)S(1)} %bitcast.270), channel_id=1, replica_groups=mesh['groups'=2,'seq_0'=8,'seq_1'=8,'expert'=2] {'seq_0','seq_1'}, dimensions={0} | all-to-all | bytes 196608 | tf_op jit(solution)/shard_map/all_to_all | solution.py:71
  309.0 4.5 %all-gather.9 = f32[2,4,96]{2,1,0:T(4,128)S(1)} all-gather(f32[1,4,96]{2,1,0:T(4,128)S(1)} %bitcast.304), channel_id=6, replica_groups=mesh['groups'=2,'seq_0'=8,'seq_1'=8,'expert'=2] {'expert'}, dimensions={0}, use_global_device_ids=true | all-gather | bytes 4608 | tf_op jit(solution)/shard_map/all_gather | solution.py:59
  313.5 0.6 reduce_sum.79
  (63 shorter events, 1.2 us)
Async XLA Ops:
  0.6 288.6 %copy-start = (bf16[2,128,6144]{2,1,0:T(8,128)(2,1)S(1)}, bf16[2,128,6144]{2,1,0:T(8,128)(2,1)}, u32[]{:S(2)}) copy-start(bf16[2,128,6144]{2,1,0:T(8,128)(2,1)} %param.23) | copy-start | bytes 9437188
  2.2 75.3 %all-to-all-start = ((bf16[2,4,3072]{2,1,0:T(4,128)(2,1)}), bf16[2,4,3072]{2,1,0:T(4,128)(2,1)S(1)}, u32[]{:S(2)}, u32[]{:S(2)}) async-start(bf16[2,4,3072]{2,1,0:T(4,128)(2,1)} %broadcast_in_dim.23), calls=%async_computation | async-start | bytes 98304 | tf_op jit(solution)/shard_map/all_to_all | solution.py:18
  77.5 7.4 %copy-start.1 = (bf16[4,3072]{1,0:T(4,128)(2,1)S(1)}, bf16[4,3072]{1,0:T(4,128)(2,1)}, u32[]{:S(2)}) copy-start(bf16[4,3072]{1,0:T(4,128)(2,1)} %param.13) | copy-start | bytes 73732
  77.5 7.5 %copy-start.2 = (bf16[2,4,512]{2,1,0:T(4,128)(2,1)S(1)}, bf16[2,4,512]{2,1,0:T(4,128)(2,1)}, u32[]{:S(2)}) copy-start(bf16[2,4,512]{2,1,0:T(4,128)(2,1)} %param.14) | copy-start | bytes 24580
  77.5 8.7 %copy-start.4 = (s32[4]{0:T(128)S(1)}, s32[4]{0:T(128)}, u32[]{:S(2)}) copy-start(s32[4]{0:T(128)} %param.16) | copy-start | bytes 52
  77.5 58.4 %all-to-all-start.1 = ((bf16[64,2,8192]{2,1,0:T(2,128)(2,1)}), bf16[64,2,8192]{2,1,0:T(2,128)(2,1)}, u32[]{:S(2)}, u32[]{:S(2)}) async-start(bf16[64,2,8192]{2,1,0:T(2,128)(2,1)} %reshape.1033), calls=%async_computation.1 | async-start | bytes 4194304 | tf_op jit(solution)/shard_map/all_to_all | solution.py:132
  263.5 29.4 %copy-start.3 = (bf16[4,96]{1,0:T(4,128)(2,1)}, bf16[4,96]{1,0:T(4,128)(2,1)S(1)}, u32[]{:S(2)}) copy-start(bf16[4,96]{1,0:T(4,128)(2,1)S(1)} %add_convert_fusion) | copy-start | bytes 2308
  264.2 19.5 %all-to-all-start.2 = ((bf16[64,4,96]{2,1,0:T(4,128)(2,1)}), bf16[64,4,96]{2,1,0:T(4,128)(2,1)S(1)}, u32[]{:S(2)}, u32[]{:S(2)}) async-start(bf16[64,4,96]{2,1,0:T(4,128)(2,1)} %broadcast_in_dim.26), calls=%async_computation.2 | async-start | bytes 131072 | tf_op jit(solution)/shard_map/all_to_all | solution.py:18
where the time goes:
time: 319 us; the launch traced here: 314 us
  local copies, waits for them, and re-layouts  115 us (36%)
  blocking collectives  78.8 us (25%)
  waiting for transfers between devices  57.4 us (18%)
  starting transfers between devices  40.6 us (13%)
  matrix products  12.8 us (4%)
  other arithmetic  8.37 us (3%)
    unnamed x22, local copies, waits for them, and re-layouts  68.2 us
    all_gather x3, blocking collectives, collected_together(): both, at, found = (lax.all_gather(jnp.concatenate(lines), axis), 0, {})  56.6 us
    all_to_all x1, waiting for transfers between devices, on_device(): lax.all_to_all(kv_cache, SEQ, split_axis=2, concat_axis=1, tiled=True)  48.9 us
    all_to_all x2, starting transfers between devices, from_everyone(): return lax.all_to_all(copies, axis, split_axis=0, concat_axis=0, tiled=True)  33.3 us
    all_to_all x1, blocking collectives, sum_at_owner(): lax.all_to_all(parts, axis, split_axis=0, concat_axis=0, tiled=True)  15.8 us
    all_to_all x1, local copies, waits for them, and re-layouts, on_device(): lax.all_to_all(kv_cache, SEQ, split_axis=2, concat_axis=1, tiled=True)  14.7 us
    another operation x1, local copies, waits for them, and re-layouts, partial_attention(): value_rows = relaid[1].reshape(kv_count, HD, slot_count, requests)  10.1 us
    another operation x1, local copies, waits for them, and re-layouts, partial_attention(): key_rows = relaid[0].reshape(kv_count, HD, slot_count, requests)  10.1 us
  transfers between devices with their start and end apart: 3, of which 2 were waited for; matrix products, arithmetic and copies ran while one was open for 18% of the time, Pallas kernels for 0%

commit v1 on v0

v1 whole, which is shorter than its diff:
```python
import math

import jax
import jax.numpy as jnp
from jax import lax
from jax.experimental import pallas as pl
from jax.experimental.pallas import tpu as pltpu
from jax.sharding import Mesh
from jax.sharding import PartitionSpec as P

H = 48
KVH = 8
HD = 128
PER = H // KVH
Y = "seq_0"
X = "seq_1"
SEQ = (Y, X)
E = "expert"
LANES = 128
ROWS = 8
FOLD = 4
HEADS = 4
F32 = jnp.float32
BF16 = jnp.bfloat16
LOW = -1e30
LARGEST = 6.0
SCALE = 1.0 / math.sqrt(HD)
PARAMS = pltpu.CompilerParams(vmem_limit_bytes=16 << 20)
NT = (((1,), (1,)), ((), ()))
NN = (((1,), (0,)), ((), ()))


def iota(shape, dim):
    return lax.broadcasted_iota(jnp.int32, shape, dim)


def vmem():
    return pl.BlockSpec(memory_space=pltpu.VMEM)


def exponent_per_unit(depth):
    return 80.0 / (LARGEST * LARGEST * depth * SCALE)


def near(array):
    return pltpu.with_memory_space_constraint(array, pltpu.VMEM)


def far(array):
    return pltpu.with_memory_space_constraint(array, pltpu.HBM)


def swapped(shard):
    return lax.ppermute(shard, E, [(0, 1), (1, 0)])


def to_everyone(copies, axes):
    return lax.all_to_all(copies, axes, split_axis=0, concat_axis=0, tiled=True)


def pack_kernel(q_ref, new_ref, lengths_ref, packed_ref, limit_ref, sizes_ref, sems):
    requests = q_ref.shape[0]
    own_heads = q_ref.shape[1] // (PER * HD)
    local = lax.axis_index(Y) % own_heads
    span = PER * HD
    head = pl.ds(pl.multiple_of(local * HD, LANES), HD)
    copies = [
        pltpu.make_async_copy(lengths_ref, sizes_ref, sems.at[0]),
        pltpu.make_async_copy(
            q_ref.at[:, pl.ds(pl.multiple_of(local * span, LANES), span)], packed_ref.at[:, 0:span], sems.at[1]
        ),
    ]
    for i in range(2):
        copies.append(
            pltpu.make_async_copy(
                new_ref.at[i, :, head], packed_ref.at[:, span + i * HD : span + (i + 1) * HD], sems.at[2 + i]
            )
        )
    for copy in copies:
        copy.start()
    copies[0].wait()
    which = iota((ROWS, LANES), 1) % requests
    limit = jnp.full((ROWS, LANES), sizes_ref[0], jnp.int32)
    for r in range(1, requests):
        limit = jnp.where(which == r, sizes_ref[r], limit)
    limit_ref[...] = limit
    for copy in copies[1:]:
        copy.wait()


def packed(queries, new_entries, lengths):
    requests = queries.shape[0]
    return pl.pallas_call(
        pack_kernel,
        in_specs=[pl.BlockSpec(memory_space=pltpu.HBM)] * 3,
        out_specs=[vmem()] * 2,
        out_shape=[
            pltpu.VMEM((requests, PER * HD + 2 * HD), BF16),
            pltpu.VMEM((ROWS, LANES), jnp.int32),
        ],
        scratch_shapes=[pltpu.SMEM((requests,), jnp.int32), pltpu.SemaphoreType.DMA((4,))],
        compiler_params=PARAMS,
        name="pack",
    )(far(queries), far(new_entries), far(lengths))


def score_kernel(peers, own_heads, mine_ref, other_ref, k_ref, kv_ref, s_ref, own_ref, v_ref, rows_ref, sem):
    requests = mine_ref.shape[0]
    depth = k_ref.shape[0]
    width = k_ref.shape[1] // peers
    slim = width // FOLD
    fetch = pltpu.make_async_copy(kv_ref.at[1], v_ref, sem)
    fetch.start()
    x = lax.axis_index(X)
    mine = (lax.axis_index(Y) // own_heads) == lax.axis_index(E)
    q = jnp.where(mine, mine_ref[...].astype(F32), other_ref[...].astype(F32))
    rows_ref[...] = jnp.zeros_like(rows_ref)
    for r in range(requests):
        for t in range(PER):
            rows_ref[r * ROWS + t : r * ROWS + t + 1, :] = q[r : r + 1, t * HD : (t + 1) * HD]
    fresh = [q[:, (PER + i) * HD : (PER + i + 1) * HD].astype(BF16) for i in range(2)]

    rolled = pltpu.roll(rows_ref[0 : requests * ROWS, :], (HD - x * depth) % HD, 1)
    query = rolled[:, 0:depth].astype(BF16)
    which = iota((ROWS, slim), 1) % requests
    for c in range(peers):
        folds = []
        for k in range(FOLD):
            at = c * width + k * slim
            found = lax.dot_general(query, k_ref[:, at : at + slim], NN, preferred_element_type=F32)
            score = found[0:ROWS]
            for r in range(1, requests):
                score = jnp.where(which == r, found[r * ROWS : (r + 1) * ROWS], score)
            folds.append(score[0:PER])
        power = jnp.concatenate(folds, axis=0) * (SCALE * exponent_per_unit(depth))
        s_ref[c] = jnp.exp(power).astype(BF16)

    rows = rows_ref[...].astype(BF16)
    every = lax.dot_general(fresh[0], rows, NT, preferred_element_type=F32)
    own_row = iota(every.shape, 1) // ROWS == iota(every.shape, 0)
    score = jnp.sum(jnp.where(own_row, every, 0.0), axis=0, keepdims=True) * SCALE
    pick = (iota((depth, HD), 1) == iota((depth, HD), 0) + x * depth).astype(BF16)
    values = lax.dot_general(pick, fresh[1], NT, preferred_element_type=F32).astype(BF16)
    spread = (iota((requests, LANES), 1) // ROWS == iota((requests, LANES), 0)).astype(BF16)
    own_ref[0:depth, :] = lax.dot_general(values, spread, NN, preferred_element_type=F32)
    line = iota((ROWS, LANES), 0)
    own_ref[depth : depth + ROWS, :] = jnp.where(line == 0, 1.0, jnp.where(line == 1, score, 0.0))
    fetch.wait()


def key_kernel(kv_ref, k_ref, sem):
    fetch = pltpu.make_async_copy(kv_ref.at[0], k_ref, sem)
    fetch.start()
    fetch.wait()


def fetched_keys(kv_cache):
    return pl.pallas_call(
        key_kernel,
        in_specs=[pl.BlockSpec(memory_space=pltpu.HBM)],
        out_specs=vmem(),
        out_shape=pltpu.VMEM(kv_cache.shape[1:], BF16),
        scratch_shapes=[pltpu.SemaphoreType.DMA],
        compiler_params=PARAMS,
        name="keys",
    )(far(kv_cache))


def partial_scores(mine, other, keys, kv_cache):
    depth = kv_cache.shape[1]
    peers = lax.axis_size(X)
    own_heads = KVH // lax.axis_size(E)
    slim = kv_cache.shape[2] // peers // FOLD
    return pl.pallas_call(
        lambda *refs: score_kernel(peers, own_heads, *refs),
        in_specs=[vmem()] * 3 + [pl.BlockSpec(memory_space=pltpu.HBM)],
        out_specs=[vmem()] * 3,
        out_shape=[
            pltpu.VMEM((peers, FOLD * PER, slim), BF16),
            pltpu.VMEM((depth + ROWS, LANES), F32),
            pltpu.VMEM(kv_cache.shape[1:], BF16),
        ],
        scratch_shapes=[pltpu.VMEM((LANES, HD), F32), pltpu.SemaphoreType.DMA],
        compiler_params=PARAMS,
        name="scores",
    )(near(mine), near(other), near(keys), far(kv_cache))


def weight_kernel(requests, half_ctx, parts_ref, limit_ref, w_ref):
    peers, tall, slim = parts_ref.shape
    blocks = slim // LANES
    start = lax.axis_index(E) * half_ctx + lax.axis_index(X) * (FOLD * slim // requests)
    limit = jnp.concatenate([limit_ref[...]] * (tall // ROWS), axis=0)
    place = iota((tall, LANES), 1) // requests + start + (iota((tall, LANES), 0) // PER) * (slim // requests)
    scores = []
    high = jnp.full((tall, LANES), LOW, F32)
    for j in range(blocks):
        at = slice(j * LANES, (j + 1) * LANES)
        total = jnp.log(parts_ref[0, :, at].astype(F32))
        for c in range(1, peers):
            total = total + jnp.log(parts_ref[c, :, at].astype(F32))
        alive = place + j * (LANES // requests) < limit
        total = jnp.where(alive, total * (1.0 / exponent_per_unit(HD // peers)), LOW)
        scores.append(total)
        high = jnp.maximum(high, total)
    best = high[0:PER]
    for k in range(1, FOLD):
        best = jnp.maximum(best, high[k * PER : (k + 1) * PER])
    step = requests
    while step < LANES:
        best = jnp.maximum(best, pltpu.roll(best, step, 1))
        step *= 2
    best16 = best.astype(BF16)
    best = best16.astype(F32)
    high = jnp.concatenate([best] * FOLD, axis=0)
    shown = jnp.concatenate([best, jnp.zeros((ROWS - PER, LANES), F32)], axis=0).astype(BF16)
    groups = tall // ROWS
    for j in range(blocks):
        alive = place + j * (LANES // requests) < limit
        weight = jnp.where(alive, jnp.exp(scores[j] - high), 0.0)
        for i in range(groups):
            tile = weight[i * ROWS : (i + 1) * ROWS].astype(BF16)
            for c in range(peers):
                w_ref[c, j * groups + i] = tile
    for c in range(peers):
        w_ref[c, blocks * groups] = shown


def local_weights(parts, limit, requests, half_ctx):
    peers, tall, slim = parts.shape
    tiles = (tall // ROWS) * (slim // LANES) + 1
    return pl.pallas_call(
        lambda *refs: weight_kernel(requests, half_ctx, *refs),
        in_specs=[vmem()] * 2,
        out_specs=vmem(),
        out_shape=pltpu.VMEM((peers, tiles, ROWS, LANES), BF16),
        compiler_params=PARAMS,
        name="weights",
    )(near(parts), near(limit))


def value_kernel(requests, w_ref, v_ref, out_ref):
    peers, tiles = w_ref.shape[:2]
    depth = v_ref.shape[0]
    slim = v_ref.shape[1] // peers // FOLD
    blocks = slim // LANES
    groups = (tiles - 1) // blocks
    used = requests * ROWS
    tops = [w_ref[c, tiles - 1].astype(F32) for c in range(peers)]
    best = tops[0]
    for c in range(1, peers):
        best = jnp.maximum(best, tops[c])
    which = iota((ROWS, slim), 1) % requests
    spare = jnp.zeros((ROWS - PER, slim), F32)
    ones = jnp.ones((depth, slim), BF16)
    acc = jnp.zeros((2 * depth, used), F32)
    for c in range(peers):
        fade = jnp.concatenate([jnp.exp(tops[c] - best)[0:PER]] * FOLD, axis=0)
        weight = jnp.concatenate(
            [
                jnp.concatenate([w_ref[c, j * groups + i].astype(F32) for i in range(groups)], axis=0) * fade
                for j in range(blocks)
            ],
            axis=1,
        )
        for k in range(FOLD):
            part = jnp.concatenate([weight[k * PER : (k + 1) * PER], spare], axis=0)
            masked = jnp.concatenate([jnp.where(which == r, part, 0.0) for r in range(requests)], axis=0)
            at = (c * FOLD + k) * slim
            values = jnp.concatenate([v_ref[:, at : at + slim], ones], axis=0)
            acc = acc + lax.dot_general(values, masked.astype(BF16), NT, preferred_element_type=F32)
    lane = iota((ROWS, LANES), 1)
    line = iota((ROWS, LANES), 0)
    mixed = jnp.where((lane // requests == line) & (lane < used), best, 0.0)
    row = jnp.broadcast_to(jnp.sum(mixed, axis=0, keepdims=True), (ROWS, LANES)).astype(BF16)
    a, b = iota((LANES, LANES), 0), iota((LANES, LANES), 1)
    moved = ((a // requests == b % ROWS) & (a % requests == b // ROWS)).astype(BF16)
    top = lax.dot_general(row, moved, NN, preferred_element_type=F32)
    out_ref[...] = jnp.zeros_like(out_ref)
    out_ref[0 : depth + ROWS, 0:used] = acc[0 : depth + ROWS]
    out_ref[depth : depth + ROWS, :] = jnp.where(line == 1, top, out_ref[depth : depth + ROWS, :])


def weighted_values(weights, values, requests):
    depth = values.shape[0]
    return pl.pallas_call(
        lambda *refs: value_kernel(requests, *refs),
        in_specs=[vmem()] * 2,
        out_specs=vmem(),
        out_shape=pltpu.VMEM((depth + ROWS, LANES), F32),
        compiler_params=PARAMS,
        name="values",
    )(near(weights), near(values))


def merge_kernel(own_ref, left_ref, right_ref, out_ref):
    depth = own_ref.shape[0] - ROWS
    parts = (own_ref, left_ref, right_ref)
    highs = [p[depth + 1 : depth + 2, :] for p in parts]
    high = jnp.maximum(jnp.maximum(highs[0], highs[1]), highs[2])
    total = jnp.zeros((1, LANES), F32)
    summed = jnp.zeros((depth, LANES), F32)
    for part, top in zip(parts, highs):
        fade = jnp.exp(top - high)
        total = total + part[depth : depth + 1, :] * fade
        summed = summed + part[0:depth, :] * fade
    attn = summed / total
    held = jnp.zeros((ROWS, LANES), F32)
    for b in range(depth // ROWS):
        held = held + pltpu.roll(attn[b * ROWS : (b + 1) * ROWS], b * (LANES // HEADS), 1)
    held = held.astype(BF16)
    for k in range(out_ref.shape[0]):
        out_ref[k] = held


def merged(own, left, right, copies):
    return pl.pallas_call(
        merge_kernel,
        in_specs=[vmem()] * 3,
        out_specs=vmem(),
        out_shape=pltpu.VMEM((copies, ROWS, LANES), BF16),
        compiler_params=PARAMS,
        name="merge",
    )(near(own), near(left), near(right))


def project_kernel(requests, attn_ref, w_ref, out_ref):
    width = w_ref.shape[0]
    heads = w_ref.shape[1] // (PER * HD)
    along = attn_ref.shape[0] // KVH
    blocks = HD // along // ROWS
    part = LANES // HEADS
    start = lax.axis_index(E) * (heads * along)
    pieces = [
        attn_ref[pl.ds(start + g * along, along)].astype(F32).reshape(along * ROWS, LANES) for g in range(heads)
    ]
    group = iota((along * ROWS, LANES), 1) // part
    stacked = []
    for b in range(blocks):
        mixed = jnp.zeros((along * ROWS, LANES), F32)
        for g in range(heads):
            mixed = jnp.where(group == g, pltpu.roll(pieces[g], ((g - b) * part) % LANES, 1), mixed)
        stacked.append(mixed)
    mixed = jnp.concatenate(stacked, axis=0).astype(BF16)
    d, k = iota((HD, HD), 0), iota((HD, HD), 1)
    order = (
        (d // (blocks * ROWS) == (k // ROWS) % along)
        & ((d // ROWS) % blocks == k // (along * ROWS))
        & (d % ROWS == k % ROWS)
    ).astype(BF16)
    attn = lax.dot_general(order, mixed, NN, preferred_element_type=F32).astype(BF16)
    lane = iota((width, LANES), 1)
    total = jnp.zeros((width, LANES), F32)
    for t in range(PER):
        for g in range(heads):
            at = g * PER * HD + t * HD
            term = lax.dot_general(w_ref[:, at : at + HD], attn, NN, preferred_element_type=F32)
            total = jnp.where((lane % ROWS == t) & (lane // part == g), term, total)
    place = iota((ROWS, LANES), 1)
    fold = ((place % part) // ROWS == iota((ROWS, LANES), 0)) & (place % ROWS < PER)
    folded = lax.dot_general(
        fold.astype(F32), total, NT, preferred_element_type=F32, precision=lax.Precision.HIGHEST
    )
    out_ref[...] = folded[0:requests, :]


def projected(attn, w_out, requests):
    return pl.pallas_call(
        lambda *refs: project_kernel(requests, *refs),
        in_specs=[vmem()] * 2,
        out_specs=vmem(),
        out_shape=pltpu.VMEM((requests, w_out.shape[1]), F32),
        compiler_params=PARAMS,
        name="project",
    )(near(attn), near(w_out.T))


def attend_kernel(residual_ref, left_ref, right_ref, out_ref, copies_ref):
    attended = (residual_ref[...].astype(F32) + (left_ref[...] + right_ref[...])).astype(BF16)
    out_ref[...] = attended
    for k in range(copies_ref.shape[0]):
        copies_ref[k] = attended


def attend(residual, left, right, copies):
    return pl.pallas_call(
        attend_kernel,
        in_specs=[vmem()] * 3,
        out_specs=[vmem()] * 2,
        out_shape=[
            pltpu.VMEM(residual.shape, BF16),
            pltpu.VMEM((copies, *residual.shape), BF16),
        ],
        compiler_params=PARAMS,
        name="attend",
    )(near(residual), near(left), near(right))


def expert_kernel(x_ref, gain_ref, router_ref, routing_ref, gate_ref, up_ref, down_ref, out_ref):
    requests = x_ref.shape[1]
    model = gain_ref.shape[0]
    held, _, hidden = gate_ref.shape
    experts_all = router_ref.shape[0]
    blocks, _, width = out_ref.shape
    widened = jnp.concatenate([x_ref[k].astype(F32) for k in range(blocks)], axis=1)
    mean_square = jnp.sum(widened * widened, axis=-1, keepdims=True) * (1.0 / model)
    normed = (widened * lax.rsqrt(mean_square + 1e-05) * gain_ref[...].astype(F32).reshape(1, model)).astype(BF16)
    row = iota((requests, experts_all), 0)
    column = iota((requests, experts_all), 1)
    exact = normed.astype(F32)
    logits = jnp.zeros((requests, experts_all), F32)
    for k in range(experts_all):
        logit = jnp.sum(exact * router_ref[k : k + 1, :].astype(F32), axis=-1, keepdims=True)
        logits = jnp.where(column == k, logit, logits)
    picked = []
    for k in range(2):
        chosen = jnp.full((requests, experts_all), routing_ref[k, 0], jnp.int32)
        for r in range(1, requests):
            chosen = jnp.where(row == r, routing_ref[k, r], chosen)
        picked.append(chosen == column)
    ahead = [jnp.sum(jnp.where(p, logits, 0.0), axis=-1, keepdims=True) for p in picked]
    first = jax.nn.sigmoid(ahead[0] - ahead[1])
    combine = jnp.where(picked[0], first, 0.0) + jnp.where(picked[1], 1.0 - first, 0.0)
    core = lax.axis_index(E)
    active = []
    for k in range(held):
        share = jnp.sum(jnp.where(column == core * held + k, combine, 0.0), axis=-1, keepdims=True)
        gate = lax.dot_general(normed, gate_ref[k], NN, preferred_element_type=F32)
        up = lax.dot_general(normed, up_ref[k], NN, preferred_element_type=F32)
        active.append((jax.nn.silu(gate) * up * share).astype(BF16))
    activation = jnp.concatenate(active, axis=-1)
    down = down_ref[...].reshape(held * hidden, model)
    terms = lax.dot_general(activation, down, NN, preferred_element_type=F32)
    for k in range(blocks):
        out_ref[k] = terms[:, k * width : (k + 1) * width]


def experts(gathered, norm_gain, router, routing, w_gate, w_up, w_down, seq_count):
    requests = gathered.shape[1]
    model = norm_gain.shape[0]
    return pl.pallas_call(
        expert_kernel,
        in_specs=[vmem()] * 3 + [pl.BlockSpec(memory_space=pltpu.SMEM)] + [vmem()] * 3,
        out_specs=vmem(),
        out_shape=pltpu.VMEM((seq_count, requests, model // seq_count), F32),
        compiler_params=PARAMS,
        name="experts",
    )(
        near(gathered),
        near(norm_gain),
        near(router.T),
        routing.T,
        near(w_gate),
        near(w_up),
        near(w_down),
    )


def on_device(
    residual,
    queries,
    new_entries,
    kv_cache,
    lengths,
    routing,
    w_out,
    norm_gain,
    router,
    w_gate,
    w_up,
    w_down,
):
    requests = lengths.shape[0]
    seq_count = lax.axis_size(SEQ)
    half_ctx = kv_cache.shape[2] // requests
    mine, limit = packed(queries, new_entries, lengths)
    scores, own, values = partial_scores(mine, swapped(mine), fetched_keys(kv_cache), kv_cache)
    scores, w_gate, w_up, w_down = lax.optimization_barrier((scores, w_gate, w_up, w_down))
    weights = local_weights(to_everyone(scores, X), limit, requests, half_ctx)
    part = weighted_values(to_everyone(weights, X), values, requests)
    attn = merged(own, part, swapped(part), seq_count)
    head_terms = projected(to_everyone(attn, SEQ), w_out, requests)
    attended, copies = attend(residual, head_terms, swapped(head_terms), seq_count)
    gathered = to_everyone(copies, SEQ)
    blocks = experts(gathered, norm_gain, router, routing, w_gate, w_up, w_down, seq_count)
    reduced = to_everyone(blocks, SEQ).sum(axis=0)
    expert_out = (reduced + swapped(reduced)).astype(BF16)
    return (attended, expert_out)


def solution(mesh):
    along_x = mesh.shape["seq"] // KVH
    split = Mesh(
        mesh.devices.reshape(mesh.shape["groups"], KVH, along_x, mesh.shape["expert"]),
        ("groups", Y, X, E),
    )
    return jax.shard_map(
        on_device,
        mesh=split,
        in_specs=(
            P("groups", SEQ),
            P("groups", E),
            P(None, "groups", E),
            P(None, SEQ, ("groups", E)),
            P("groups"),
            P("groups", None),
            P(E, SEQ),
            P(),
            P(),
            P(E, None, SEQ),
            P(E, None, SEQ),
            P(E, SEQ, None),
        ),
        out_specs=(P("groups", SEQ), P("groups", SEQ)),
        check_vma=False,
    )
```

time: 319 us -> 122 us (0.38); the launches traced: 314 us -> 121 us
  local copies, waits for them, and re-layouts: 115 us -> 0.61 us
  waiting for transfers between devices: 57.4 us -> 1.92 us
  starting transfers between devices: 40.6 us -> 26.7 us
  matrix products: 12.8 us -> 0 us
  Pallas kernels: 0 us -> 8.62 us
  other arithmetic: 8.37 us -> 0.64 us
  blocking collectives: 78.8 us -> 82.2 us
    unnamed x22 -> x17, local copies, waits for them, and re-layouts: 68.2 us -> 0.61 us
    all_to_all x1 -> x5, blocking collectives: 15.8 us -> 82.2 us  [to_everyone(): return lax.all_to_all(copies, axes, split_axis=0, concat_axis=0, tiled=True)]
    all_gather x5 -> x0, blocking collectives: 63 us -> none  [the longest x3 56.6 us: collected_together(): both, at, found = (lax.all_gather(jnp.concatenate(lines), axis), 0, {})]
    all_to_all x3 -> x0, waiting for transfers between devices: 57.4 us -> none  [the longest x1 48.9 us: on_device(): lax.all_to_all(kv_cache, SEQ, split_axis=2, concat_axis=1, tiled=True)]
    all_to_all x3 -> x0, starting transfers between devices: 40.6 us -> none  [the longest x2 33.3 us: from_everyone(): return lax.all_to_all(copies, axis, split_axis=0, concat_axis=0, tiled=True)]
    ppermute x0 -> x4, starting transfers between devices: none -> 26.7 us  [swapped(): return lax.ppermute(shard, E, [(0, 1), (1, 0)])]
    another operation x4 -> x0, local copies, waits for them, and re-layouts: 20.3 us -> none  [the longest x1 10.1 us: partial_attention(): value_rows = relaid[1].reshape(kv_count, HD, slot_count, requests)]
    all_to_all x1 -> x0, local copies, waits for them, and re-layouts: 14.7 us -> none  [on_device(): lax.all_to_all(kv_cache, SEQ, split_axis=2, concat_axis=1, tiled=True)]
  transfers between devices with their start and end apart: 3 -> 4, of which waited for: 2 -> 3; matrix products, arithmetic and copies ran while one was open for 18% -> 0% of each run, Pallas kernels for 0% -> 1%
where the time goes in v1:
time: 122 us; the launch traced here: 121 us
  blocking collectives  82.2 us (67%)
  starting transfers between devices  26.7 us (22%)
  Pallas kernels  8.62 us (7%)
  waiting for transfers between devices  1.92 us (2%)
    all_to_all x5, blocking collectives, to_everyone(): return lax.all_to_all(copies, axes, split_axis=0, concat_axis=0, tiled=True)  82.2 us
    ppermute x4, starting transfers between devices, swapped(): return lax.ppermute(shard, E, [(0, 1), (1, 0)])  26.7 us
  transfers between devices with their start and end apart: 4, of which 3 were waited for; matrix products, arithmetic and copies ran while one was open for 0% of the time, Pallas kernels for 1%

profile of v1, /device:TPU:513, one launch (start us, length us, event | category | flops | bytes accessed | tf_op | source)
XLA Modules:
  0.0 121.5 jit_solution(15972257509784966556)
XLA Ops:
  0.6 0.8 pack.1
  1.4 20.5 %collective-permute-start = (bf16[4,1024]{1,0:T(4,128)(2,1)S(1)}, bf16[4,1024]{1,0:T(4,128)(2,1)S(1)}, u32[]{:S(2)}, u32[]{:S(2)}) collective-permute-start(bf16[4,1024]{1,0:T(4,128)(2,1)S(1)} %get-tuple-element.13.refs_0_), channel_id=1, source_target_pairs={{0,1},{1,0},{2,3},{3,2},{4,5},{5,4},{6,7},{7,6},{8,9},{9,8},{10,11... | collective-permute-start | bytes 24584 | tf_op jit(solution)/shard_map/ppermute | solution.py:54
  21.9 0.0 copy-start.2
  21.9 1.4 %keys.1.refs_2_ = bf16[16,32768]{1,0:T(8,128)(2,1)S(1)} custom-call(bf16[2,16,32768]{2,1,0:T(8,128)(2,1)} %refs_3_.1), custom_call_target="tpu_custom_call" | custom-call | tf_op jit(solution)/shard_map/keys/pallas_call | solution.py:158
  23.3 0.0 copy-start.3
  23.3 0.0 collective-permute-done.refs_1_
  23.4 0.0 copy-start.1
  23.4 2.1 %scores.1 = (bf16[8,24,1024]{2,1,0:T(8,128)(2,1)S(1)}, f32[24,128]{1,0:T(8,128)S(1)}, bf16[16,32768]{1,0:T(8,128)(2,1)S(1)}) custom-call(bf16[4,1024]{1,0:T(4,128)(2,1)S(1)} %get-tuple-element.13.refs_0_, bf16[4,1024]{1,0:T(4,128)(2,1)S(1)} %collective-permute-done.refs_1_, bf16[16,32768]{1,0:T(8,128)(2,1)S(1)} %keys.1.refs_2_, bf16[2,16,32768]{2,1,0:T(8,128)(2,1)} %refs_3_.1), custom_call_target="tpu_custom_call" | custom-call | tf_op jit(solution)/shard_map/scores/pallas_call | solution.py:174
  25.5 0.0 copy-start.6
  25.5 0.0 copy-start
  25.5 0.0 copy-start.4
  25.5 0.0 copy-start.5
  25.5 0.0 copy-start.7
  25.5 17.8 %all_to_all.25.refs_0_ = bf16[8,24,1024]{2,1,0:T(8,128)(2,1)S(1)} all-to-all(bf16[8,24,1024]{2,1,0:T(8,128)(2,1)S(1)} %get-tuple-element.16), channel_id=1, replica_groups=mesh['groups'=2,'seq_0'=8,'seq_1'=8,'expert'=2] {'seq_1'}, dimensions={0} | all-to-all | bytes 786432 | tf_op jit(solution)/shard_map/all_to_all | solution.py:58
  43.4 0.5 weights.1
  43.9 17.1 %all_to_all.26.refs_0_ = bf16[8,25,8,128]{3,2,1,0:T(8,128)(2,1)S(1)} all-to-all(bf16[8,25,8,128]{3,2,1,0:T(8,128)(2,1)S(1)} %weights.1), channel_id=1, replica_groups=mesh['groups'=2,'seq_0'=8,'seq_1'=8,'expert'=2] {'seq_1'}, dimensions={0} | all-to-all | bytes 819200 | tf_op jit(solution)/shard_map/all_to_all | solution.py:58
  61.0 0.7 values.1.left_ref
  61.8 1.4 %collective-permute-start.1 = (f32[24,128]{1,0:T(8,128)S(1)}, f32[24,128]{1,0:T(8,128)S(1)}, u32[]{:S(2)}, u32[]{:S(2)}) collective-permute-start(f32[24,128]{1,0:T(8,128)S(1)} %values.1.left_ref), channel_id=1, source_target_pairs={{0,1},{1,0},{2,3},{3,2},{4,5},{5,4},{6,7},{7,6},{8,9},{9,8},{10,11... | collective-permute-start | bytes 36872 | tf_op jit(solution)/shard_map/ppermute | solution.py:54
  63.2 0.8 collective-permute-done.1.right_ref
  64.0 0.1 merge.1
  64.1 15.9 %all_to_all.27.refs_0_ = bf16[64,8,128]{2,1,0:T(8,128)(2,1)S(1)} all-to-all(bf16[64,8,128]{2,1,0:T(8,128)(2,1)S(1)} %merge.1), channel_id=1, replica_groups=mesh['groups'=2,'seq_0'=8,'seq_1'=8,'expert'=2] {'seq_0','seq_1'}, dimensions={0} | all-to-all | bytes 262144 | tf_op jit(solution)/shard_map/all_to_all | solution.py:58
  80.0 0.0 copy-done.3
  80.0 0.7 project.1.left_ref
  80.7 2.0 %collective-permute-start.2 = (f32[4,96]{1,0:T(4,128)S(1)}, f32[4,96]{1,0:T(4,128)S(1)}, u32[]{:S(2)}, u32[]{:S(2)}) collective-permute-start(f32[4,96]{1,0:T(4,128)S(1)} %project.1.left_ref), channel_id=1, source_target_pairs={{0,1},{1,0},{2,3},{3,2},{4,5},{5,4},{6,7},{7,6},{8,9},{9,8},{10,11... | collective-permute-start | bytes 4616 | tf_op jit(solution)/shard_map/ppermute | solution.py:54
  82.7 0.8 collective-permute-done.2.right_ref
  83.5 0.0 copy-done.6
  83.6 15.5 %all_to_all.28.x_ref = bf16[64,4,96]{2,1,0:T(4,128)(2,1)S(1)} all-to-all(bf16[64,4,96]{2,1,0:T(4,128)(2,1)S(1)} %get-tuple-element.20), channel_id=1, replica_groups=mesh['groups'=2,'seq_0'=8,'seq_1'=8,'expert'=2] {'seq_0','seq_1'}, dimensions={0} | all-to-all | bytes 98304 | tf_op jit(solution)/shard_map/all_to_all | solution.py:58
  99.1 0.0 copy-done.2
  99.1 0.0 copy-done.1
  99.1 0.0 copy-done
  99.1 0.0 copy-done.4
  99.1 0.0 copy-done.5
  99.1 0.0 copy-done.7
  99.2 2.3 %experts.1 = f32[64,4,96]{2,1,0:T(4,128)S(1)} custom-call(bf16[64,4,96]{2,1,0:T(4,128)(2,1)S(1)} %all_to_all.28.x_ref, bf16[6144]{0:T(1024)(128)(2,1)S(1)} %copy-done.5, bf16[4,6144]{1,0:T(4,128)(2,1)S(1)} %bitcast.4, s32[2,4]{1,0:T(2,128)S(1)} %bitcast.5, bf16[2,6144,128]{2,1,0:T(8,128)(2,1)S(1)} %copy-done, bf16[2,6144,128]{2,1,0:T(8,128)(2,1)S(1)} %copy-done.1, ...), custom_call_target="tpu_custom_call" | custom-call | tf_op jit(solution)/shard_map/experts/pallas_call | solution.py:441
  101.4 15.8 %all_to_all.29 = f32[64,4,96]{2,1,0:T(4,128)S(1)} all-to-all(f32[64,4,96]{2,1,0:T(4,128)S(1)} %experts.1), channel_id=1, replica_groups=mesh['groups'=2,'seq_0'=8,'seq_1'=8,'expert'=2] {'seq_0','seq_1'}, dimensions={0} | all-to-all | bytes 196608 | tf_op jit(solution)/shard_map/all_to_all | solution.py:58
  117.3 0.1 reduce_sum.9
  117.4 2.7 %collective-permute-start.3 = (f32[4,96]{1,0:T(4,128)S(1)}, f32[4,96]{1,0:T(4,128)S(1)}, u32[]{:S(2)}, u32[]{:S(2)}) collective-permute-start(f32[4,96]{1,0:T(4,128)S(1)} %reduce_sum.9), channel_id=1, source_target_pairs={{0,1},{1,0},{2,3},{3,2},{4,5},{5,4},{6,7},{7,6},{8,9},{9,8},{10,11... | collective-permute-start | bytes 4616 | tf_op jit(solution)/shard_map/ppermute | solution.py:54
  120.1 0.6 copy.14
  120.7 0.3 collective-permute-done.3
  120.9 0.6 add_convert_fusion
  (1 shorter events, 0.0 us)
Async XLA Ops:
  1.4 21.9 %collective-permute-start = (bf16[4,1024]{1,0:T(4,128)(2,1)S(1)}, bf16[4,1024]{1,0:T(4,128)(2,1)S(1)}, u32[]{:S(2)}, u32[]{:S(2)}) collective-permute-start(bf16[4,1024]{1,0:T(4,128)(2,1)S(1)} %get-tuple-element.13.refs_0_), channel_id=1, source_target_pairs={{0,1},{1,0},{2,3},{3,2},{4,5},{5,4},{6,7},{7,6},{8,9},{9,8},{10,11... | collective-permute-start | bytes 24584 | tf_op jit(solution)/shard_map/ppermute | solution.py:54
  21.9 77.2 %copy-start.2 = (bf16[2,128,6144]{2,1,0:T(8,128)(2,1)S(1)}, bf16[2,128,6144]{2,1,0:T(8,128)(2,1)}, u32[]{:S(2)}) copy-start(bf16[2,128,6144]{2,1,0:T(8,128)(2,1)} %down_ref) | copy-start | bytes 9437188
  23.3 56.7 %copy-start.3 = (bf16[3072,96]{0,1:T(8,128)(2,1)S(1)}, bf16[3072,96]{0,1:T(8,128)(2,1)}, u32[]{:S(2)}) copy-start(bf16[3072,96]{0,1:T(8,128)(2,1)} %param.18) | copy-start | bytes 1769476
  23.4 75.8 %copy-start.1 = (bf16[2,6144,128]{2,1,0:T(8,128)(2,1)S(1)}, bf16[2,6144,128]{2,1,0:T(8,128)(2,1)}, u32[]{:S(2)}) copy-start(bf16[2,6144,128]{2,1,0:T(8,128)(2,1)} %up_ref) | copy-start | bytes 9437188
  25.5 58.1 %copy-start.6 = (bf16[4,96]{1,0:T(4,128)(2,1)S(1)}, bf16[4,96]{1,0:T(4,128)(2,1)}, u32[]{:S(2)}) copy-start(bf16[4,96]{1,0:T(4,128)(2,1)} %residual_ref.1) | copy-start | bytes 2308
  25.5 73.6 %copy-start = (bf16[2,6144,128]{2,1,0:T(8,128)(2,1)S(1)}, bf16[2,6144,128]{2,1,0:T(8,128)(2,1)}, u32[]{:S(2)}) copy-start(bf16[2,6144,128]{2,1,0:T(8,128)(2,1)} %gate_ref) | copy-start | bytes 9437188
  25.5 73.6 %copy-start.4 = (bf16[6144,4]{0,1:T(4,128)(2,1)S(1)}, bf16[6144,4]{0,1:T(4,128)(2,1)}, u32[]{:S(2)}) copy-start(bf16[6144,4]{0,1:T(4,128)(2,1)} %param.20) | copy-start | bytes 147460
  25.5 73.6 %copy-start.5 = (bf16[6144]{0:T(1024)(128)(2,1)S(1)}, bf16[6144]{0:T(1024)(128)(2,1)}, u32[]{:S(2)}) copy-start(bf16[6144]{0:T(1024)(128)(2,1)} %gain_ref.1) | copy-start | bytes 36868
  25.5 73.6 %copy-start.7 = (s32[4,2]{0,1:T(2,128)S(1)}, s32[4,2]{0,1:T(2,128)}, u32[]{:S(2)}) copy-start(s32[4,2]{0,1:T(2,128)} %param.17) | copy-start | bytes 100
  61.8 2.3 %collective-permute-start.1 = (f32[24,128]{1,0:T(8,128)S(1)}, f32[24,128]{1,0:T(8,128)S(1)}, u32[]{:S(2)}, u32[]{:S(2)}) collective-permute-start(f32[24,128]{1,0:T(8,128)S(1)} %values.1.left_ref), channel_id=1, source_target_pairs={{0,1},{1,0},{2,3},{3,2},{4,5},{5,4},{6,7},{7,6},{8,9},{9,8},{10,11... | collective-permute-start | bytes 36872 | tf_op jit(solution)/shard_map/ppermute | solution.py:54
  80.7 2.8 %collective-permute-start.2 = (f32[4,96]{1,0:T(4,128)S(1)}, f32[4,96]{1,0:T(4,128)S(1)}, u32[]{:S(2)}, u32[]{:S(2)}) collective-permute-start(f32[4,96]{1,0:T(4,128)S(1)} %project.1.left_ref), channel_id=1, source_target_pairs={{0,1},{1,0},{2,3},{3,2},{4,5},{5,4},{6,7},{7,6},{8,9},{9,8},{10,11... | collective-permute-start | bytes 4616 | tf_op jit(solution)/shard_map/ppermute | solution.py:54
  117.4 3.6 %collective-permute-start.3 = (f32[4,96]{1,0:T(4,128)S(1)}, f32[4,96]{1,0:T(4,128)S(1)}, u32[]{:S(2)}, u32[]{:S(2)}) collective-permute-start(f32[4,96]{1,0:T(4,128)S(1)} %reduce_sum.9), channel_id=1, source_target_pairs={{0,1},{1,0},{2,3},{3,2},{4,5},{5,4},{6,7},{7,6},{8,9},{9,8},{10,11... | collective-permute-start | bytes 4616 | tf_op jit(solution)/shard_map/ppermute | solution.py:54

commit v2 on v1

--- a/solution.py
+++ b/solution.py
@@ -104,13 +104,11 @@
     )(far(queries), far(new_entries), far(lengths))
 
 
-def score_kernel(peers, own_heads, mine_ref, other_ref, k_ref, kv_ref, s_ref, own_ref, v_ref, rows_ref, sem):
+def score_kernel(peers, own_heads, mine_ref, other_ref, k_ref, s_ref, own_ref, rows_ref):
     requests = mine_ref.shape[0]
     depth = k_ref.shape[0]
     width = k_ref.shape[1] // peers
     slim = width // FOLD
-    fetch = pltpu.make_async_copy(kv_ref.at[1], v_ref, sem)
-    fetch.start()
     x = lax.axis_index(X)
     mine = (lax.axis_index(Y) // own_heads) == lax.axis_index(E)
     q = jnp.where(mine, mine_ref[...].astype(F32), other_ref[...].astype(F32))
@@ -145,7 +143,6 @@
     own_ref[0:depth, :] = lax.dot_general(values, spread, NN, preferred_element_type=F32)
     line = iota((ROWS, LANES), 0)
     own_ref[depth : depth + ROWS, :] = jnp.where(line == 0, 1.0, jnp.where(line == 1, score, 0.0))
-    fetch.wait()
 
 
 def key_kernel(kv_ref, k_ref, sem):
@@ -166,24 +163,20 @@
     )(far(kv_cache))
 
 
-def partial_scores(mine, other, keys, kv_cache):
-    depth = kv_cache.shape[1]
+def partial_scores(mine, other, keys):
+    depth = keys.shape[0]
     peers = lax.axis_size(X)
     own_heads = KVH // lax.axis_size(E)
-    slim = kv_cache.shape[2] // peers // FOLD
+    slim = keys.shape[1] // peers // FOLD
     return pl.pallas_call(
         lambda *refs: score_kernel(peers, own_heads, *refs),
-        in_specs=[vmem()] * 3 + [pl.BlockSpec(memory_space=pltpu.HBM)],
-        out_specs=[vmem()] * 3,
-        out_shape=[
-            pltpu.VMEM((peers, FOLD * PER, slim), BF16),
-            pltpu.VMEM((depth + ROWS, LANES), F32),
-            pltpu.VMEM(kv_cache.shape[1:], BF16),
-        ],
-        scratch_shapes=[pltpu.VMEM((LANES, HD), F32), pltpu.SemaphoreType.DMA],
+        in_specs=[vmem()] * 3,
+        out_specs=[vmem()] * 2,
+        out_shape=[pltpu.VMEM((peers, FOLD * PER, slim), BF16), pltpu.VMEM((depth + ROWS, LANES), F32)],
+        scratch_shapes=[pltpu.VMEM((LANES, HD), F32)],
         compiler_params=PARAMS,
         name="scores",
-    )(near(mine), near(other), near(keys), far(kv_cache))
+    )(near(mine), near(other), near(keys))
 
 
 def weight_kernel(requests, half_ctx, parts_ref, limit_ref, w_ref):
@@ -241,8 +234,8 @@
 
 def value_kernel(requests, w_ref, v_ref, out_ref):
     peers, tiles = w_ref.shape[:2]
-    depth = v_ref.shape[0]
-    slim = v_ref.shape[1] // peers // FOLD
+    depth = v_ref.shape[1]
+    slim = v_ref.shape[2] // peers // FOLD
     blocks = slim // LANES
     groups = (tiles - 1) // blocks
     used = requests * ROWS
@@ -267,7 +260,7 @@
             part = jnp.concatenate([weight[k * PER : (k + 1) * PER], spare], axis=0)
             masked = jnp.concatenate([jnp.where(which == r, part, 0.0) for r in range(requests)], axis=0)
             at = (c * FOLD + k) * slim
-            values = jnp.concatenate([v_ref[:, at : at + slim], ones], axis=0)
+            values = jnp.concatenate([v_ref[1, :, at : at + slim], ones], axis=0)
             acc = acc + lax.dot_general(values, masked.astype(BF16), NT, preferred_element_type=F32)
     lane = iota((ROWS, LANES), 1)
     line = iota((ROWS, LANES), 0)
@@ -281,8 +274,8 @@
     out_ref[depth : depth + ROWS, :] = jnp.where(line == 1, top, out_ref[depth : depth + ROWS, :])
 
 
-def weighted_values(weights, values, requests):
-    depth = values.shape[0]
+def weighted_values(weights, kv_cache, requests):
+    depth = kv_cache.shape[1]
     return pl.pallas_call(
         lambda *refs: value_kernel(requests, *refs),
         in_specs=[vmem()] * 2,
@@ -290,7 +283,7 @@
         out_shape=pltpu.VMEM((depth + ROWS, LANES), F32),
         compiler_params=PARAMS,
         name="values",
-    )(near(weights), near(values))
+    )(near(weights), near(kv_cache))
 
 
 def merge_kernel(own_ref, left_ref, right_ref, out_ref):
@@ -396,7 +389,9 @@
     )(near(residual), near(left), near(right))
 
 
-def expert_kernel(x_ref, gain_ref, router_ref, routing_ref, gate_ref, up_ref, down_ref, out_ref):
+def expert_kernel(x_ref, gain_ref, router_ref, routing_ref, gate_ref, up_ref, far_ref, out_ref, down_ref, sem):
+    fetch = pltpu.make_async_copy(far_ref, down_ref, sem)
+    fetch.start()
     requests = x_ref.shape[1]
     model = gain_ref.shape[0]
     held, _, hidden = gate_ref.shape
@@ -429,6 +424,7 @@
         up = lax.dot_general(normed, up_ref[k], NN, preferred_element_type=F32)
         active.append((jax.nn.silu(gate) * up * share).astype(BF16))
     activation = jnp.concatenate(active, axis=-1)
+    fetch.wait()
     down = down_ref[...].reshape(held * hidden, model)
     terms = lax.dot_general(activation, down, NN, preferred_element_type=F32)
     for k in range(blocks):
@@ -440,8 +436,14 @@
     model = norm_gain.shape[0]
     return pl.pallas_call(
         expert_kernel,
-        in_specs=[vmem()] * 3 + [pl.BlockSpec(memory_space=pltpu.SMEM)] + [vmem()] * 3,
+        in_specs=[
+            *[vmem()] * 3,
+            pl.BlockSpec(memory_space=pltpu.SMEM),
+            *[vmem()] * 2,
+            pl.BlockSpec(memory_space=pltpu.HBM),
+        ],
         out_specs=vmem(),
+        scratch_shapes=[pltpu.VMEM(w_down.shape, BF16), pltpu.SemaphoreType.DMA],
         out_shape=pltpu.VMEM((seq_count, requests, model // seq_count), F32),
         compiler_params=PARAMS,
         name="experts",
@@ -452,7 +454,7 @@
         routing.T,
         near(w_gate),
         near(w_up),
-        near(w_down),
+        far(w_down),
     )
 
 
@@ -474,10 +476,9 @@
     seq_count = lax.axis_size(SEQ)
     half_ctx = kv_cache.shape[2] // requests
     mine, limit = packed(queries, new_entries, lengths)
-    scores, own, values = partial_scores(mine, swapped(mine), fetched_keys(kv_cache), kv_cache)
-    scores, w_gate, w_up, w_down = lax.optimization_barrier((scores, w_gate, w_up, w_down))
+    scores, own = partial_scores(mine, swapped(mine), fetched_keys(kv_cache))
     weights = local_weights(to_everyone(scores, X), limit, requests, half_ctx)
-    part = weighted_values(to_everyone(weights, X), values, requests)
+    part = weighted_values(to_everyone(weights, X), kv_cache, requests)
     attn = merged(own, part, swapped(part), seq_count)
     head_terms = projected(to_everyone(attn, SEQ), w_out, requests)
     attended, copies = attend(residual, head_terms, swapped(head_terms), seq_count)

time: 122 us -> 122 us (level)
    pallas_call x1, Pallas kernels: 2.28 us -> 4.11 us  [experts(): pl.pallas_call(expert_kernel, in_specs=[*[vmem()] * 3, pl.BlockSpec(memor...]
where the time goes in v2:
time: 122 us
  blocking collectives  82.2 us (67%)
  starting transfers between devices  26.7 us (22%)
  Pallas kernels  9.08 us (7%)
  waiting for transfers between devices  1.92 us (2%)
    all_to_all x5, blocking collectives, to_everyone(): return lax.all_to_all(copies, axes, split_axis=0, concat_axis=0, tiled=True)  82.2 us
    ppermute x4, starting transfers between devices, swapped(): return lax.ppermute(shard, E, [(0, 1), (1, 0)])  26.7 us
    pallas_call x1, Pallas kernels, experts(): pl.pallas_call(expert_kernel, in_specs=[*[vmem()] * 3, pl.BlockSpec(memor...  4.11 us
  transfers between devices with their start and end apart: 4, of which 3 were waited for; matrix products, arithmetic and copies ran while one was open for 0% of the time, Pallas kernels for 1%

profile of v2, /device:TPU:513, one launch (start us, length us, event | category | flops | bytes accessed | tf_op | source)
XLA Modules:
  0.0 121.9 jit_solution(5317868075744579238)
XLA Ops:
  0.6 0.8 pack.1
  1.4 0.0 copy-start
  1.4 20.5 %collective-permute-start = (bf16[4,1024]{1,0:T(4,128)(2,1)S(1)}, bf16[4,1024]{1,0:T(4,128)(2,1)S(1)}, u32[]{:S(2)}, u32[]{:S(2)}) collective-permute-start(bf16[4,1024]{1,0:T(4,128)(2,1)S(1)} %get-tuple-element.8.refs_0_), channel_id=1, source_target_pairs={{0,1},{1,0},{2,3},{3,2},{4,5},{5,4},{6,7},{7,6},{8,9},{9,8},{10,11... | collective-permute-start | bytes 24584 | tf_op jit(solution)/shard_map/ppermute | solution.py:54
  21.9 1.2 %keys.1.refs_2_ = bf16[16,32768]{1,0:T(8,128)(2,1)S(1)} custom-call(bf16[2,16,32768]{2,1,0:T(8,128)(2,1)} %refs_1_.1), custom_call_target="tpu_custom_call" | custom-call | tf_op jit(solution)/shard_map/keys/pallas_call | solution.py:155
  23.2 0.0 copy-start.3
  23.2 0.0 collective-permute-done.refs_1_
  23.2 0.0 copy-start.2
  23.2 0.9 scores.1
  24.1 0.0 copy-start.6
  24.1 0.0 copy-start.1
  24.1 0.0 copy-start.4
  24.1 0.0 copy-start.5
  24.1 0.0 copy-start.7
  24.2 17.8 %all_to_all.25.refs_0_ = bf16[8,24,1024]{2,1,0:T(8,128)(2,1)S(1)} all-to-all(bf16[8,24,1024]{2,1,0:T(8,128)(2,1)S(1)} %get-tuple-element.10), channel_id=1, replica_groups=mesh['groups'=2,'seq_0'=8,'seq_1'=8,'expert'=2] {'seq_1'}, dimensions={0} | all-to-all | bytes 786432 | tf_op jit(solution)/shard_map/all_to_all | solution.py:58
  42.0 0.5 weights.1
  42.5 17.1 %all_to_all.26.refs_0_ = bf16[8,25,8,128]{3,2,1,0:T(8,128)(2,1)S(1)} all-to-all(bf16[8,25,8,128]{3,2,1,0:T(8,128)(2,1)S(1)} %weights.1), channel_id=1, replica_groups=mesh['groups'=2,'seq_0'=8,'seq_1'=8,'expert'=2] {'seq_1'}, dimensions={0} | all-to-all | bytes 819200 | tf_op jit(solution)/shard_map/all_to_all | solution.py:58
  59.7 0.0 copy-done
  59.7 0.7 values.1.left_ref
  60.4 1.4 %collective-permute-start.1 = (f32[24,128]{1,0:T(8,128)S(1)}, f32[24,128]{1,0:T(8,128)S(1)}, u32[]{:S(2)}, u32[]{:S(2)}) collective-permute-start(f32[24,128]{1,0:T(8,128)S(1)} %values.1.left_ref), channel_id=1, source_target_pairs={{0,1},{1,0},{2,3},{3,2},{4,5},{5,4},{6,7},{7,6},{8,9},{9,8},{10,11... | collective-permute-start | bytes 36872 | tf_op jit(solution)/shard_map/ppermute | solution.py:54
  61.8 0.8 collective-permute-done.1.right_ref
  62.6 0.1 merge.1
  62.7 15.9 %all_to_all.27.refs_0_ = bf16[64,8,128]{2,1,0:T(8,128)(2,1)S(1)} all-to-all(bf16[64,8,128]{2,1,0:T(8,128)(2,1)S(1)} %merge.1), channel_id=1, replica_groups=mesh['groups'=2,'seq_0'=8,'seq_1'=8,'expert'=2] {'seq_0','seq_1'}, dimensions={0} | all-to-all | bytes 262144 | tf_op jit(solution)/shard_map/all_to_all | solution.py:58
  78.6 0.0 copy-done.3
  78.6 0.7 project.1.left_ref
  79.3 2.0 %collective-permute-start.2 = (f32[4,96]{1,0:T(4,128)S(1)}, f32[4,96]{1,0:T(4,128)S(1)}, u32[]{:S(2)}, u32[]{:S(2)}) collective-permute-start(f32[4,96]{1,0:T(4,128)S(1)} %project.1.left_ref), channel_id=1, source_target_pairs={{0,1},{1,0},{2,3},{3,2},{4,5},{5,4},{6,7},{7,6},{8,9},{9,8},{10,11... | collective-permute-start | bytes 4616 | tf_op jit(solution)/shard_map/ppermute | solution.py:54
  81.3 0.8 collective-permute-done.2.right_ref
  82.2 0.0 copy-done.6
  82.2 15.5 %all_to_all.28.x_ref = bf16[64,4,96]{2,1,0:T(4,128)(2,1)S(1)} all-to-all(bf16[64,4,96]{2,1,0:T(4,128)(2,1)S(1)} %get-tuple-element.13), channel_id=1, replica_groups=mesh['groups'=2,'seq_0'=8,'seq_1'=8,'expert'=2] {'seq_0','seq_1'}, dimensions={0} | all-to-all | bytes 98304 | tf_op jit(solution)/shard_map/all_to_all | solution.py:58
  97.7 0.0 copy-done.2
  97.7 0.0 copy-done.1
  97.7 0.0 copy-done.4
  97.7 0.0 copy-done.5
  97.8 0.0 copy-done.7
  97.8 4.1 %experts.1 = f32[64,4,96]{2,1,0:T(4,128)S(1)} custom-call(bf16[64,4,96]{2,1,0:T(4,128)(2,1)S(1)} %all_to_all.28.x_ref, bf16[6144]{0:T(1024)(128)(2,1)S(1)} %copy-done.5, bf16[4,6144]{1,0:T(4,128)(2,1)S(1)} %bitcast.4, s32[2,4]{1,0:T(2,128)S(1)} %bitcast.5, bf16[2,6144,128]{2,1,0:T(8,128)(2,1)S(1)} %copy-done.1, bf16[2,6144,128]{2,1,0:T(8,128)(2,1)S(1)} %copy-done.2, ...), custom_call_target="tpu_custom_call" | custom-call | tf_op jit(solution)/shard_map/experts/pallas_call | solution.py:437
  101.9 15.8 %all_to_all.29 = f32[64,4,96]{2,1,0:T(4,128)S(1)} all-to-all(f32[64,4,96]{2,1,0:T(4,128)S(1)} %experts.1), channel_id=1, replica_groups=mesh['groups'=2,'seq_0'=8,'seq_1'=8,'expert'=2] {'seq_0','seq_1'}, dimensions={0} | all-to-all | bytes 196608 | tf_op jit(solution)/shard_map/all_to_all | solution.py:58
  117.7 0.1 reduce_sum.9
  117.8 2.7 %collective-permute-start.3 = (f32[4,96]{1,0:T(4,128)S(1)}, f32[4,96]{1,0:T(4,128)S(1)}, u32[]{:S(2)}, u32[]{:S(2)}) collective-permute-start(f32[4,96]{1,0:T(4,128)S(1)} %reduce_sum.9), channel_id=1, source_target_pairs={{0,1},{1,0},{2,3},{3,2},{4,5},{5,4},{6,7},{7,6},{8,9},{9,8},{10,11... | collective-permute-start | bytes 4616 | tf_op jit(solution)/shard_map/ppermute | solution.py:54
  120.5 0.6 copy.14
  121.1 0.3 collective-permute-done.3
  121.3 0.6 add_convert_fusion
  (1 shorter events, 0.0 us)
Async XLA Ops:
  1.4 58.3 %copy-start = (bf16[2,16,32768]{2,1,0:T(8,128)(2,1)S(1)}, bf16[2,16,32768]{2,1,0:T(8,128)(2,1)}, u32[]{:S(2)}) copy-start(bf16[2,16,32768]{2,1,0:T(8,128)(2,1)} %refs_1_.1) | copy-start | bytes 6291460
  1.4 21.8 %collective-permute-start = (bf16[4,1024]{1,0:T(4,128)(2,1)S(1)}, bf16[4,1024]{1,0:T(4,128)(2,1)S(1)}, u32[]{:S(2)}, u32[]{:S(2)}) collective-permute-start(bf16[4,1024]{1,0:T(4,128)(2,1)S(1)} %get-tuple-element.8.refs_0_), channel_id=1, source_target_pairs={{0,1},{1,0},{2,3},{3,2},{4,5},{5,4},{6,7},{7,6},{8,9},{9,8},{10,11... | collective-permute-start | bytes 24584 | tf_op jit(solution)/shard_map/ppermute | solution.py:54
  23.2 55.4 %copy-start.3 = (bf16[3072,96]{0,1:T(8,128)(2,1)S(1)}, bf16[3072,96]{0,1:T(8,128)(2,1)}, u32[]{:S(2)}) copy-start(bf16[3072,96]{0,1:T(8,128)(2,1)} %param.18) | copy-start | bytes 1769476
  23.2 74.5 %copy-start.2 = (bf16[2,6144,128]{2,1,0:T(8,128)(2,1)S(1)}, bf16[2,6144,128]{2,1,0:T(8,128)(2,1)}, u32[]{:S(2)}) copy-start(bf16[2,6144,128]{2,1,0:T(8,128)(2,1)} %up_ref.1) | copy-start | bytes 9437188
  24.1 58.0 %copy-start.6 = (bf16[4,96]{1,0:T(4,128)(2,1)S(1)}, bf16[4,96]{1,0:T(4,128)(2,1)}, u32[]{:S(2)}) copy-start(bf16[4,96]{1,0:T(4,128)(2,1)} %residual_ref.1) | copy-start | bytes 2308
  24.1 73.6 %copy-start.1 = (bf16[2,6144,128]{2,1,0:T(8,128)(2,1)S(1)}, bf16[2,6144,128]{2,1,0:T(8,128)(2,1)}, u32[]{:S(2)}) copy-start(bf16[2,6144,128]{2,1,0:T(8,128)(2,1)} %gate_ref.1) | copy-start | bytes 9437188
  24.1 73.6 %copy-start.4 = (bf16[6144,4]{0,1:T(4,128)(2,1)S(1)}, bf16[6144,4]{0,1:T(4,128)(2,1)}, u32[]{:S(2)}) copy-start(bf16[6144,4]{0,1:T(4,128)(2,1)} %param.20) | copy-start | bytes 147460
  24.1 73.6 %copy-start.5 = (bf16[6144]{0:T(1024)(128)(2,1)S(1)}, bf16[6144]{0:T(1024)(128)(2,1)}, u32[]{:S(2)}) copy-start(bf16[6144]{0:T(1024)(128)(2,1)} %gain_ref.1) | copy-start | bytes 36868
  24.1 73.6 %copy-start.7 = (s32[4,2]{0,1:T(2,128)S(1)}, s32[4,2]{0,1:T(2,128)}, u32[]{:S(2)}) copy-start(s32[4,2]{0,1:T(2,128)} %param.17) | copy-start | bytes 100
  60.4 2.3 %collective-permute-start.1 = (f32[24,128]{1,0:T(8,128)S(1)}, f32[24,128]{1,0:T(8,128)S(1)}, u32[]{:S(2)}, u32[]{:S(2)}) collective-permute-start(f32[24,128]{1,0:T(8,128)S(1)} %values.1.left_ref), channel_id=1, source_target_pairs={{0,1},{1,0},{2,3},{3,2},{4,5},{5,4},{6,7},{7,6},{8,9},{9,8},{10,11... | collective-permute-start | bytes 36872 | tf_op jit(solution)/shard_map/ppermute | solution.py:54
  79.3 2.8 %collective-permute-start.2 = (f32[4,96]{1,0:T(4,128)S(1)}, f32[4,96]{1,0:T(4,128)S(1)}, u32[]{:S(2)}, u32[]{:S(2)}) collective-permute-start(f32[4,96]{1,0:T(4,128)S(1)} %project.1.left_ref), channel_id=1, source_target_pairs={{0,1},{1,0},{2,3},{3,2},{4,5},{5,4},{6,7},{7,6},{8,9},{9,8},{10,11... | collective-permute-start | bytes 4616 | tf_op jit(solution)/shard_map/ppermute | solution.py:54
  117.8 3.6 %collective-permute-start.3 = (f32[4,96]{1,0:T(4,128)S(1)}, f32[4,96]{1,0:T(4,128)S(1)}, u32[]{:S(2)}, u32[]{:S(2)}) collective-permute-start(f32[4,96]{1,0:T(4,128)S(1)} %reduce_sum.9), channel_id=1, source_target_pairs={{0,1},{1,0},{2,3},{3,2},{4,5},{5,4},{6,7},{7,6},{8,9},{9,8},{10,11... | collective-permute-start | bytes 4616 | tf_op jit(solution)/shard_map/ppermute | solution.py:54

commit v3 on v1

--- a/solution.py
+++ b/solution.py
@@ -58,7 +58,7 @@
     return lax.all_to_all(copies, axes, split_axis=0, concat_axis=0, tiled=True)
 
 
-def pack_kernel(q_ref, new_ref, lengths_ref, packed_ref, limit_ref, sizes_ref, sems):
+def pack_kernel(q_ref, new_ref, lengths_ref, kv_ref, packed_ref, limit_ref, k_ref, sizes_ref, sems):
     requests = q_ref.shape[0]
     own_heads = q_ref.shape[1] // (PER * HD)
     local = lax.axis_index(Y) % own_heads
@@ -76,6 +76,7 @@
                 new_ref.at[i, :, head], packed_ref.at[:, span + i * HD : span + (i + 1) * HD], sems.at[2 + i]
             )
         )
+    copies.append(pltpu.make_async_copy(kv_ref.at[0], k_ref, sems.at[4]))
     for copy in copies:
         copy.start()
     copies[0].wait()
@@ -88,29 +89,28 @@
         copy.wait()
 
 
-def packed(queries, new_entries, lengths):
+def packed(queries, new_entries, lengths, kv_cache):
     requests = queries.shape[0]
     return pl.pallas_call(
         pack_kernel,
-        in_specs=[pl.BlockSpec(memory_space=pltpu.HBM)] * 3,
-        out_specs=[vmem()] * 2,
+        in_specs=[pl.BlockSpec(memory_space=pltpu.HBM)] * 4,
+        out_specs=[vmem()] * 3,
         out_shape=[
             pltpu.VMEM((requests, PER * HD + 2 * HD), BF16),
             pltpu.VMEM((ROWS, LANES), jnp.int32),
+            pltpu.VMEM(kv_cache.shape[1:], BF16),
         ],
-        scratch_shapes=[pltpu.SMEM((requests,), jnp.int32), pltpu.SemaphoreType.DMA((4,))],
+        scratch_shapes=[pltpu.SMEM((requests,), jnp.int32), pltpu.SemaphoreType.DMA((5,))],
         compiler_params=PARAMS,
         name="pack",
-    )(far(queries), far(new_entries), far(lengths))
-
-
-def score_kernel(peers, own_heads, mine_ref, other_ref, k_ref, kv_ref, s_ref, own_ref, v_ref, rows_ref, sem):
+    )(far(queries), far(new_entries), far(lengths), far(kv_cache))
+
+
+def score_kernel(peers, own_heads, mine_ref, other_ref, k_ref, s_ref, own_ref, rows_ref):
     requests = mine_ref.shape[0]
     depth = k_ref.shape[0]
     width = k_ref.shape[1] // peers
     slim = width // FOLD
-    fetch = pltpu.make_async_copy(kv_ref.at[1], v_ref, sem)
-    fetch.start()
     x = lax.axis_index(X)
     mine = (lax.axis_index(Y) // own_heads) == lax.axis_index(E)
     q = jnp.where(mine, mine_ref[...].astype(F32), other_ref[...].astype(F32))
@@ -145,45 +145,40 @@
     own_ref[0:depth, :] = lax.dot_general(values, spread, NN, preferred_element_type=F32)
     line = iota((ROWS, LANES), 0)
     own_ref[depth : depth + ROWS, :] = jnp.where(line == 0, 1.0, jnp.where(line == 1, score, 0.0))
-    fetch.wait()
-
-
-def key_kernel(kv_ref, k_ref, sem):
-    fetch = pltpu.make_async_copy(kv_ref.at[0], k_ref, sem)
+
+
+def value_fetch_kernel(kv_ref, v_ref, sem):
+    fetch = pltpu.make_async_copy(kv_ref.at[1], v_ref, sem)
     fetch.start()
     fetch.wait()
 
 
-def fetched_keys(kv_cache):
-    return pl.pallas_call(
-        key_kernel,
+def fetched_values(kv_cache):
+    return pl.pallas_call(
+        value_fetch_kernel,
         in_specs=[pl.BlockSpec(memory_space=pltpu.HBM)],
         out_specs=vmem(),
         out_shape=pltpu.VMEM(kv_cache.shape[1:], BF16),
         scratch_shapes=[pltpu.SemaphoreType.DMA],
         compiler_params=PARAMS,
-        name="keys",
+        name="fetch_values",
     )(far(kv_cache))
 
 
-def partial_scores(mine, other, keys, kv_cache):
-    depth = kv_cache.shape[1]
+def partial_scores(mine, other, keys):
+    depth = keys.shape[0]
     peers = lax.axis_size(X)
     own_heads = KVH // lax.axis_size(E)
-    slim = kv_cache.shape[2] // peers // FOLD
+    slim = keys.shape[1] // peers // FOLD
     return pl.pallas_call(
         lambda *refs: score_kernel(peers, own_heads, *refs),
-        in_specs=[vmem()] * 3 + [pl.BlockSpec(memory_space=pltpu.HBM)],
-        out_specs=[vmem()] * 3,
-        out_shape=[
-            pltpu.VMEM((peers, FOLD * PER, slim), BF16),
-            pltpu.VMEM((depth + ROWS, LANES), F32),
-            pltpu.VMEM(kv_cache.shape[1:], BF16),
-        ],
-        scratch_shapes=[pltpu.VMEM((LANES, HD), F32), pltpu.SemaphoreType.DMA],
+        in_specs=[vmem()] * 3,
+        out_specs=[vmem()] * 2,
+        out_shape=[pltpu.VMEM((peers, FOLD * PER, slim), BF16), pltpu.VMEM((depth + ROWS, LANES), F32)],
+        scratch_shapes=[pltpu.VMEM((LANES, HD), F32)],
         compiler_params=PARAMS,
         name="scores",
-    )(near(mine), near(other), near(keys), far(kv_cache))
+    )(near(mine), near(other), near(keys))
 
 
 def weight_kernel(requests, half_ctx, parts_ref, limit_ref, w_ref):
@@ -473,9 +468,11 @@
     requests = lengths.shape[0]
     seq_count = lax.axis_size(SEQ)
     half_ctx = kv_cache.shape[2] // requests
-    mine, limit = packed(queries, new_entries, lengths)
-    scores, own, values = partial_scores(mine, swapped(mine), fetched_keys(kv_cache), kv_cache)
-    scores, w_gate, w_up, w_down = lax.optimization_barrier((scores, w_gate, w_up, w_down))
+    mine, limit, keys = packed(queries, new_entries, lengths, kv_cache)
+    other = swapped(mine)
+    values = fetched_values(kv_cache)
+    other, values = lax.optimization_barrier((other, values))
+    scores, own = partial_scores(mine, other, keys)
     weights = local_weights(to_everyone(scores, X), limit, requests, half_ctx)
     part = weighted_values(to_everyone(weights, X), values, requests)
     attn = merged(own, part, swapped(part), seq_count)

time: 122 us -> 121 us (level)
  no operation moved by 1% of the time
where the time goes in v3:
time: 121 us
  blocking collectives  82.1 us (68%)
  starting transfers between devices  26.7 us (22%)
  Pallas kernels  8.12 us (7%)
  waiting for transfers between devices  1.92 us (2%)
    all_to_all x5, blocking collectives, to_everyone(): return lax.all_to_all(copies, axes, split_axis=0, concat_axis=0, tiled=True)  82.1 us
    ppermute x4, starting transfers between devices, swapped(): return lax.ppermute(shard, E, [(0, 1), (1, 0)])  26.7 us
  transfers between devices with their start and end apart: 4, of which 3 were waited for; matrix products, arithmetic and copies ran while one was open for 0% of the time, Pallas kernels for 1%

profile of v3, /device:TPU:513, one launch (start us, length us, event | category | flops | bytes accessed | tf_op | source)
XLA Modules:
  0.0 120.8 jit_solution(10352734895901105489)
XLA Ops:
  0.6 0.0 copy-start.2
  0.6 1.5 %pack.1 = (bf16[4,1024]{1,0:T(4,128)(2,1)S(1)}, s32[8,128]{1,0:T(8,128)S(1)}, bf16[16,32768]{1,0:T(8,128)(2,1)S(1)}) custom-call(bf16[4,3072]{1,0:T(4,128)(2,1)} %q_ref.1, bf16[2,4,512]{2,1,0:T(4,128)(2,1)} %new_ref.1, s32[4]{0:T(128)} %lengths_ref.1, bf16[2,16,32768]{2,1,0:T(8,128)(2,1)} %kv_ref.3), custom_call_target="tpu_custom_call" | custom-call | tf_op jit(solution)/shard_map/pack/pallas_call | solution.py:94
  2.1 20.5 %collective-permute-start = (bf16[4,1024]{1,0:T(4,128)(2,1)S(1)}, bf16[4,1024]{1,0:T(4,128)(2,1)S(1)}, u32[]{:S(2)}, u32[]{:S(2)}) collective-permute-start(bf16[4,1024]{1,0:T(4,128)(2,1)S(1)} %get-tuple-element.11.refs_0_), channel_id=1, source_target_pairs={{0,1},{1,0},{2,3},{3,2},{4,5},{5,4},{6,7},{7,6},{8,9},{9,8},{10,11... | collective-permute-start | bytes 24584 | tf_op jit(solution)/shard_map/ppermute | solution.py:54
  22.7 0.0 copy-start.1
  22.7 1.4 %fetch_values.1.refs_1_ = bf16[16,32768]{1,0:T(8,128)(2,1)S(1)} custom-call(bf16[2,16,32768]{2,1,0:T(8,128)(2,1)} %kv_ref.3), custom_call_target="tpu_custom_call" | custom-call | tf_op jit(solution)/shard_map/fetch_values/pallas_call | solution.py:157
  24.1 0.0 copy-start.3
  24.1 0.0 copy-start.6
  24.1 0.0 copy-start
  24.1 0.0 copy-start.4
  24.1 0.0 copy-start.5
  24.1 0.0 copy-start.7
  24.1 0.0 collective-permute-done.refs_1_
  24.1 0.9 scores.1
  25.0 17.7 %all_to_all.25.refs_0_ = bf16[8,24,1024]{2,1,0:T(8,128)(2,1)S(1)} all-to-all(bf16[8,24,1024]{2,1,0:T(8,128)(2,1)S(1)} %get-tuple-element.15), channel_id=1, replica_groups=mesh['groups'=2,'seq_0'=8,'seq_1'=8,'expert'=2] {'seq_1'}, dimensions={0} | all-to-all | bytes 786432 | tf_op jit(solution)/shard_map/all_to_all | solution.py:58
  42.7 0.5 weights.1
  43.3 17.1 %all_to_all.26.refs_0_ = bf16[8,25,8,128]{3,2,1,0:T(8,128)(2,1)S(1)} all-to-all(bf16[8,25,8,128]{3,2,1,0:T(8,128)(2,1)S(1)} %weights.1), channel_id=1, replica_groups=mesh['groups'=2,'seq_0'=8,'seq_1'=8,'expert'=2] {'seq_1'}, dimensions={0} | all-to-all | bytes 819200 | tf_op jit(solution)/shard_map/all_to_all | solution.py:58
  60.4 0.7 values.1.left_ref
  61.1 1.4 %collective-permute-start.1 = (f32[24,128]{1,0:T(8,128)S(1)}, f32[24,128]{1,0:T(8,128)S(1)}, u32[]{:S(2)}, u32[]{:S(2)}) collective-permute-start(f32[24,128]{1,0:T(8,128)S(1)} %values.1.left_ref), channel_id=1, source_target_pairs={{0,1},{1,0},{2,3},{3,2},{4,5},{5,4},{6,7},{7,6},{8,9},{9,8},{10,11... | collective-permute-start | bytes 36872 | tf_op jit(solution)/shard_map/ppermute | solution.py:54
  62.5 0.8 collective-permute-done.1.right_ref
  63.4 0.1 merge.1
  63.5 15.9 %all_to_all.27.refs_0_ = bf16[64,8,128]{2,1,0:T(8,128)(2,1)S(1)} all-to-all(bf16[64,8,128]{2,1,0:T(8,128)(2,1)S(1)} %merge.1), channel_id=1, replica_groups=mesh['groups'=2,'seq_0'=8,'seq_1'=8,'expert'=2] {'seq_0','seq_1'}, dimensions={0} | all-to-all | bytes 262144 | tf_op jit(solution)/shard_map/all_to_all | solution.py:58
  79.3 0.0 copy-done.3
  79.3 0.7 project.1.left_ref
  80.1 2.0 %collective-permute-start.2 = (f32[4,96]{1,0:T(4,128)S(1)}, f32[4,96]{1,0:T(4,128)S(1)}, u32[]{:S(2)}, u32[]{:S(2)}) collective-permute-start(f32[4,96]{1,0:T(4,128)S(1)} %project.1.left_ref), channel_id=1, source_target_pairs={{0,1},{1,0},{2,3},{3,2},{4,5},{5,4},{6,7},{7,6},{8,9},{9,8},{10,11... | collective-permute-start | bytes 4616 | tf_op jit(solution)/shard_map/ppermute | solution.py:54
  82.1 0.8 collective-permute-done.2.right_ref
  82.9 0.0 copy-done.6
  82.9 15.5 %all_to_all.28.x_ref = bf16[64,4,96]{2,1,0:T(4,128)(2,1)S(1)} all-to-all(bf16[64,4,96]{2,1,0:T(4,128)(2,1)S(1)} %get-tuple-element.19), channel_id=1, replica_groups=mesh['groups'=2,'seq_0'=8,'seq_1'=8,'expert'=2] {'seq_0','seq_1'}, dimensions={0} | all-to-all | bytes 98304 | tf_op jit(solution)/shard_map/all_to_all | solution.py:58
  98.5 0.0 copy-done.2
  98.5 0.0 copy-done.1
  98.5 0.0 copy-done
  98.5 0.0 copy-done.4
  98.5 0.0 copy-done.5
  98.5 0.0 copy-done.7
  98.5 2.3 %experts.1 = f32[64,4,96]{2,1,0:T(4,128)S(1)} custom-call(bf16[64,4,96]{2,1,0:T(4,128)(2,1)S(1)} %all_to_all.28.x_ref, bf16[6144]{0:T(1024)(128)(2,1)S(1)} %copy-done.5, bf16[4,6144]{1,0:T(4,128)(2,1)S(1)} %bitcast.4, s32[2,4]{1,0:T(2,128)S(1)} %bitcast.5, bf16[2,6144,128]{2,1,0:T(8,128)(2,1)S(1)} %copy-done, bf16[2,6144,128]{2,1,0:T(8,128)(2,1)S(1)} %copy-done.1, ...), custom_call_target="tpu_custom_call" | custom-call | tf_op jit(solution)/shard_map/experts/pallas_call | solution.py:436
  100.8 15.8 %all_to_all.29 = f32[64,4,96]{2,1,0:T(4,128)S(1)} all-to-all(f32[64,4,96]{2,1,0:T(4,128)S(1)} %experts.1), channel_id=1, replica_groups=mesh['groups'=2,'seq_0'=8,'seq_1'=8,'expert'=2] {'seq_0','seq_1'}, dimensions={0} | all-to-all | bytes 196608 | tf_op jit(solution)/shard_map/all_to_all | solution.py:58
  116.6 0.1 reduce_sum.9
  116.7 2.7 %collective-permute-start.3 = (f32[4,96]{1,0:T(4,128)S(1)}, f32[4,96]{1,0:T(4,128)S(1)}, u32[]{:S(2)}, u32[]{:S(2)}) collective-permute-start(f32[4,96]{1,0:T(4,128)S(1)} %reduce_sum.9), channel_id=1, source_target_pairs={{0,1},{1,0},{2,3},{3,2},{4,5},{5,4},{6,7},{7,6},{8,9},{9,8},{10,11... | collective-permute-start | bytes 4616 | tf_op jit(solution)/shard_map/ppermute | solution.py:54
  119.5 0.6 copy.14
  120.0 0.3 collective-permute-done.3
  120.3 0.6 add_convert_fusion
  (1 shorter events, 0.0 us)
Async XLA Ops:
  0.6 97.8 %copy-start.2 = (bf16[2,128,6144]{2,1,0:T(8,128)(2,1)S(1)}, bf16[2,128,6144]{2,1,0:T(8,128)(2,1)}, u32[]{:S(2)}) copy-start(bf16[2,128,6144]{2,1,0:T(8,128)(2,1)} %down_ref.1) | copy-start | bytes 9437188
  2.1 22.0 %collective-permute-start = (bf16[4,1024]{1,0:T(4,128)(2,1)S(1)}, bf16[4,1024]{1,0:T(4,128)(2,1)S(1)}, u32[]{:S(2)}, u32[]{:S(2)}) collective-permute-start(bf16[4,1024]{1,0:T(4,128)(2,1)S(1)} %get-tuple-element.11.refs_0_), channel_id=1, source_target_pairs={{0,1},{1,0},{2,3},{3,2},{4,5},{5,4},{6,7},{7,6},{8,9},{9,8},{10,11... | collective-permute-start | bytes 24584 | tf_op jit(solution)/shard_map/ppermute | solution.py:54
  22.7 75.8 %copy-start.1 = (bf16[2,6144,128]{2,1,0:T(8,128)(2,1)S(1)}, bf16[2,6144,128]{2,1,0:T(8,128)(2,1)}, u32[]{:S(2)}) copy-start(bf16[2,6144,128]{2,1,0:T(8,128)(2,1)} %up_ref.1) | copy-start | bytes 9437188
  24.1 55.3 %copy-start.3 = (bf16[3072,96]{0,1:T(8,128)(2,1)S(1)}, bf16[3072,96]{0,1:T(8,128)(2,1)}, u32[]{:S(2)}) copy-start(bf16[3072,96]{0,1:T(8,128)(2,1)} %param.18) | copy-start | bytes 1769476
  24.1 58.8 %copy-start.6 = (bf16[4,96]{1,0:T(4,128)(2,1)S(1)}, bf16[4,96]{1,0:T(4,128)(2,1)}, u32[]{:S(2)}) copy-start(bf16[4,96]{1,0:T(4,128)(2,1)} %residual_ref.1) | copy-start | bytes 2308
  24.1 74.4 %copy-start = (bf16[2,6144,128]{2,1,0:T(8,128)(2,1)S(1)}, bf16[2,6144,128]{2,1,0:T(8,128)(2,1)}, u32[]{:S(2)}) copy-start(bf16[2,6144,128]{2,1,0:T(8,128)(2,1)} %gate_ref.1) | copy-start | bytes 9437188
  24.1 74.4 %copy-start.4 = (bf16[6144,4]{0,1:T(4,128)(2,1)S(1)}, bf16[6144,4]{0,1:T(4,128)(2,1)}, u32[]{:S(2)}) copy-start(bf16[6144,4]{0,1:T(4,128)(2,1)} %param.20) | copy-start | bytes 147460
  24.1 74.4 %copy-start.5 = (bf16[6144]{0:T(1024)(128)(2,1)S(1)}, bf16[6144]{0:T(1024)(128)(2,1)}, u32[]{:S(2)}) copy-start(bf16[6144]{0:T(1024)(128)(2,1)} %gain_ref.1) | copy-start | bytes 36868
  24.1 74.4 %copy-start.7 = (s32[4,2]{0,1:T(2,128)S(1)}, s32[4,2]{0,1:T(2,128)}, u32[]{:S(2)}) copy-start(s32[4,2]{0,1:T(2,128)} %param.17) | copy-start | bytes 100
  61.1 2.3 %collective-permute-start.1 = (f32[24,128]{1,0:T(8,128)S(1)}, f32[24,128]{1,0:T(8,128)S(1)}, u32[]{:S(2)}, u32[]{:S(2)}) collective-permute-start(f32[24,128]{1,0:T(8,128)S(1)} %values.1.left_ref), channel_id=1, source_target_pairs={{0,1},{1,0},{2,3},{3,2},{4,5},{5,4},{6,7},{7,6},{8,9},{9,8},{10,11... | collective-permute-start | bytes 36872 | tf_op jit(solution)/shard_map/ppermute | solution.py:54
  80.1 2.8 %collective-permute-start.2 = (f32[4,96]{1,0:T(4,128)S(1)}, f32[4,96]{1,0:T(4,128)S(1)}, u32[]{:S(2)}, u32[]{:S(2)}) collective-permute-start(f32[4,96]{1,0:T(4,128)S(1)} %project.1.left_ref), channel_id=1, source_target_pairs={{0,1},{1,0},{2,3},{3,2},{4,5},{5,4},{6,7},{7,6},{8,9},{9,8},{10,11... | collective-permute-start | bytes 4616 | tf_op jit(solution)/shard_map/ppermute | solution.py:54
  116.7 3.6 %collective-permute-start.3 = (f32[4,96]{1,0:T(4,128)S(1)}, f32[4,96]{1,0:T(4,128)S(1)}, u32[]{:S(2)}, u32[]{:S(2)}) collective-permute-start(f32[4,96]{1,0:T(4,128)S(1)} %reduce_sum.9), channel_id=1, source_target_pairs={{0,1},{1,0},{2,3},{3,2},{4,5},{5,4},{6,7},{7,6},{8,9},{9,8},{10,11... | collective-permute-start | bytes 4616 | tf_op jit(solution)/shard_map/ppermute | solution.py:54

commit v4 on v3

--- a/solution.py
+++ b/solution.py
@@ -25,6 +25,7 @@
 LOW = -1e30
 LARGEST = 6.0
 SCALE = 1.0 / math.sqrt(HD)
+AFTER_TRANSFER = pl.CostEstimate(flops=20_000_000_000, transcendentals=0, bytes_accessed=1 << 24)
 PARAMS = pltpu.CompilerParams(vmem_limit_bytes=16 << 20)
 NT = (((1,), (1,)), ((), ()))
 NN = (((1,), (0,)), ((), ()))
@@ -230,6 +231,7 @@
         out_specs=vmem(),
         out_shape=pltpu.VMEM((peers, tiles, ROWS, LANES), BF16),
         compiler_params=PARAMS,
+        cost_estimate=AFTER_TRANSFER,
         name="weights",
     )(near(parts), near(limit))
 
@@ -284,6 +286,7 @@
         out_specs=vmem(),
         out_shape=pltpu.VMEM((depth + ROWS, LANES), F32),
         compiler_params=PARAMS,
+        cost_estimate=AFTER_TRANSFER,
         name="values",
     )(near(weights), near(values))
 
@@ -315,6 +318,7 @@
         out_specs=vmem(),
         out_shape=pltpu.VMEM((copies, ROWS, LANES), BF16),
         compiler_params=PARAMS,
+        cost_estimate=AFTER_TRANSFER,
         name="merge",
     )(near(own), near(left), near(right))
 
@@ -366,6 +370,7 @@
         out_specs=vmem(),
         out_shape=pltpu.VMEM((requests, w_out.shape[1]), F32),
         compiler_params=PARAMS,
+        cost_estimate=AFTER_TRANSFER,
         name="project",
     )(near(attn), near(w_out.T))
 
@@ -387,6 +392,7 @@
             pltpu.VMEM((copies, *residual.shape), BF16),
         ],
         compiler_params=PARAMS,
+        cost_estimate=AFTER_TRANSFER,
         name="attend",
     )(near(residual), near(left), near(right))
 

time: 121 us -> 121 us (level)
  no operation moved by 1% of the time
where the time goes in v4:
time: 121 us
  blocking collectives  82 us (68%)
  starting transfers between devices  27.1 us (22%)
  Pallas kernels  7.81 us (6%)
  waiting for transfers between devices  1.92 us (2%)
    all_to_all x5, blocking collectives, to_everyone(): return lax.all_to_all(copies, axes, split_axis=0, concat_axis=0, tiled=True)  82 us
    ppermute x4, starting transfers between devices, swapped(): return lax.ppermute(shard, E, [(0, 1), (1, 0)])  27.1 us
  transfers between devices with their start and end apart: 4, of which 3 were waited for; matrix products, arithmetic and copies ran while one was open for 0% of the time, Pallas kernels for 1%

profile of v4, /device:TPU:513, one launch (start us, length us, event | category | flops | bytes accessed | tf_op | source)
XLA Modules:
  0.0 120.9 jit_solution(980183882329693727)
XLA Ops:
  0.6 1.3 %pack.1 = (bf16[4,1024]{1,0:T(4,128)(2,1)S(1)}, s32[8,128]{1,0:T(8,128)S(1)}, bf16[16,32768]{1,0:T(8,128)(2,1)S(1)}) custom-call(bf16[4,3072]{1,0:T(4,128)(2,1)} %q_ref.1, bf16[2,4,512]{2,1,0:T(4,128)(2,1)} %new_ref.1, s32[4]{0:T(128)} %lengths_ref.1, bf16[2,16,32768]{2,1,0:T(8,128)(2,1)} %kv_ref.3), custom_call_target="tpu_custom_call" | custom-call | tf_op jit(solution)/shard_map/pack/pallas_call | solution.py:95
  2.0 20.5 %collective-permute-start = (bf16[4,1024]{1,0:T(4,128)(2,1)S(1)}, bf16[4,1024]{1,0:T(4,128)(2,1)S(1)}, u32[]{:S(2)}, u32[]{:S(2)}) collective-permute-start(bf16[4,1024]{1,0:T(4,128)(2,1)S(1)} %get-tuple-element.11.refs_0_), channel_id=1, source_target_pairs={{0,1},{1,0},{2,3},{3,2},{4,5},{5,4},{6,7},{7,6},{8,9},{9,8},{10,11... | collective-permute-start | bytes 24584 | tf_op jit(solution)/shard_map/ppermute | solution.py:55
  22.5 1.2 %fetch_values.1.refs_1_ = bf16[16,32768]{1,0:T(8,128)(2,1)S(1)} custom-call(bf16[2,16,32768]{2,1,0:T(8,128)(2,1)} %kv_ref.3), custom_call_target="tpu_custom_call" | custom-call | tf_op jit(solution)/shard_map/fetch_values/pallas_call | solution.py:158
  23.7 0.0 collective-permute-done.refs_1_
  23.8 0.9 scores.1
  24.7 17.6 %all_to_all.25.refs_0_ = bf16[8,24,1024]{2,1,0:T(8,128)(2,1)S(1)} all-to-all(bf16[8,24,1024]{2,1,0:T(8,128)(2,1)S(1)} %get-tuple-element.15), channel_id=1, replica_groups=mesh['groups'=2,'seq_0'=8,'seq_1'=8,'expert'=2] {'seq_1'}, dimensions={0} | all-to-all | bytes 786432 | tf_op jit(solution)/shard_map/all_to_all | solution.py:59
  42.2 0.5 weights.1
  42.8 17.1 %all_to_all.26.refs_0_ = bf16[8,25,8,128]{3,2,1,0:T(8,128)(2,1)S(1)} all-to-all(bf16[8,25,8,128]{3,2,1,0:T(8,128)(2,1)S(1)} %weights.1), channel_id=1, replica_groups=mesh['groups'=2,'seq_0'=8,'seq_1'=8,'expert'=2] {'seq_1'}, dimensions={0} | all-to-all | bytes 819200 | tf_op jit(solution)/shard_map/all_to_all | solution.py:59
  59.9 0.7 values.1.left_ref
  60.6 1.4 %collective-permute-start.1 = (f32[24,128]{1,0:T(8,128)S(1)}, f32[24,128]{1,0:T(8,128)S(1)}, u32[]{:S(2)}, u32[]{:S(2)}) collective-permute-start(f32[24,128]{1,0:T(8,128)S(1)} %values.1.left_ref), channel_id=1, source_target_pairs={{0,1},{1,0},{2,3},{3,2},{4,5},{5,4},{6,7},{7,6},{8,9},{9,8},{10,11... | collective-permute-start | bytes 36872 | tf_op jit(solution)/shard_map/ppermute | solution.py:55
  62.0 0.8 collective-permute-done.1.right_ref
  62.9 0.0 copy-start.6
  62.9 0.1 merge.1
  63.0 16.0 %all_to_all.27.refs_0_ = bf16[64,8,128]{2,1,0:T(8,128)(2,1)S(1)} all-to-all(bf16[64,8,128]{2,1,0:T(8,128)(2,1)S(1)} %merge.1), channel_id=1, replica_groups=mesh['groups'=2,'seq_0'=8,'seq_1'=8,'expert'=2] {'seq_0','seq_1'}, dimensions={0} | all-to-all | bytes 262144 | tf_op jit(solution)/shard_map/all_to_all | solution.py:59
  79.0 0.0 copy-done.6
  79.0 0.0 copy-start.7
  79.0 0.7 project.1.left_ref
  79.7 0.0 copy-start
  79.7 0.0 copy-start.1
  79.7 0.0 copy-start.2
  79.7 0.1 copy-start.3
  79.8 0.0 copy-start.4
  79.8 0.0 copy-start.5
  79.8 2.1 %collective-permute-start.2 = (f32[4,96]{1,0:T(4,128)S(1)}, f32[4,96]{1,0:T(4,128)S(1)}, u32[]{:S(2)}, u32[]{:S(2)}) collective-permute-start(f32[4,96]{1,0:T(4,128)S(1)} %project.1.left_ref), channel_id=1, source_target_pairs={{0,1},{1,0},{2,3},{3,2},{4,5},{5,4},{6,7},{7,6},{8,9},{9,8},{10,11... | collective-permute-start | bytes 4616 | tf_op jit(solution)/shard_map/ppermute | solution.py:55
  81.9 0.8 collective-permute-done.2.right_ref
  82.7 0.0 copy-done.7
  82.7 15.5 %all_to_all.28.x_ref = bf16[64,4,96]{2,1,0:T(4,128)(2,1)S(1)} all-to-all(bf16[64,4,96]{2,1,0:T(4,128)(2,1)S(1)} %get-tuple-element.19), channel_id=1, replica_groups=mesh['groups'=2,'seq_0'=8,'seq_1'=8,'expert'=2] {'seq_0','seq_1'}, dimensions={0} | all-to-all | bytes 98304 | tf_op jit(solution)/shard_map/all_to_all | solution.py:59
  98.2 0.0 copy-done
  98.3 0.0 copy-done.1
  98.3 0.0 copy-done.2
  98.3 0.0 copy-done.3
  98.3 0.0 copy-done.4
  98.3 0.0 copy-done.5
  98.3 2.3 %experts.1 = f32[64,4,96]{2,1,0:T(4,128)S(1)} custom-call(bf16[64,4,96]{2,1,0:T(4,128)(2,1)S(1)} %all_to_all.28.x_ref, bf16[6144]{0:T(1024)(128)(2,1)S(1)} %copy-done.4, bf16[4,6144]{1,0:T(4,128)(2,1)S(1)} %bitcast.3, s32[2,4]{1,0:T(2,128)S(1)} %bitcast.4, bf16[2,6144,128]{2,1,0:T(8,128)(2,1)S(1)} %copy-done, bf16[2,6144,128]{2,1,0:T(8,128)(2,1)S(1)} %copy-done.1, ...), custom_call_target="tpu_custom_call" | custom-call | tf_op jit(solution)/shard_map/experts/pallas_call | solution.py:442
  100.6 15.8 %all_to_all.29 = f32[64,4,96]{2,1,0:T(4,128)S(1)} all-to-all(f32[64,4,96]{2,1,0:T(4,128)S(1)} %experts.1), channel_id=1, replica_groups=mesh['groups'=2,'seq_0'=8,'seq_1'=8,'expert'=2] {'seq_0','seq_1'}, dimensions={0} | all-to-all | bytes 196608 | tf_op jit(solution)/shard_map/all_to_all | solution.py:59
  116.4 0.1 reduce_sum.9
  116.5 3.0 %collective-permute-start.3 = (f32[4,96]{1,0:T(4,128)S(1)}, f32[4,96]{1,0:T(4,128)S(1)}, u32[]{:S(2)}, u32[]{:S(2)}) collective-permute-start(f32[4,96]{1,0:T(4,128)S(1)} %reduce_sum.9), channel_id=1, source_target_pairs={{0,1},{1,0},{2,3},{3,2},{4,5},{5,4},{6,7},{7,6},{8,9},{9,8},{10,11... | collective-permute-start | bytes 4616 | tf_op jit(solution)/shard_map/ppermute | solution.py:55
  119.5 0.6 copy.14
  120.1 0.3 collective-permute-done.3
  120.3 0.6 add_convert_fusion
  (1 shorter events, 0.0 us)
Async XLA Ops:
  2.0 21.8 %collective-permute-start = (bf16[4,1024]{1,0:T(4,128)(2,1)S(1)}, bf16[4,1024]{1,0:T(4,128)(2,1)S(1)}, u32[]{:S(2)}, u32[]{:S(2)}) collective-permute-start(bf16[4,1024]{1,0:T(4,128)(2,1)S(1)} %get-tuple-element.11.refs_0_), channel_id=1, source_target_pairs={{0,1},{1,0},{2,3},{3,2},{4,5},{5,4},{6,7},{7,6},{8,9},{9,8},{10,11... | collective-permute-start | bytes 24584 | tf_op jit(solution)/shard_map/ppermute | solution.py:55
  60.6 2.3 %collective-permute-start.1 = (f32[24,128]{1,0:T(8,128)S(1)}, f32[24,128]{1,0:T(8,128)S(1)}, u32[]{:S(2)}, u32[]{:S(2)}) collective-permute-start(f32[24,128]{1,0:T(8,128)S(1)} %values.1.left_ref), channel_id=1, source_target_pairs={{0,1},{1,0},{2,3},{3,2},{4,5},{5,4},{6,7},{7,6},{8,9},{9,8},{10,11... | collective-permute-start | bytes 36872 | tf_op jit(solution)/shard_map/ppermute | solution.py:55
  62.9 16.1 %copy-start.6 = (bf16[3072,96]{0,1:T(8,128)(2,1)S(1)}, bf16[3072,96]{0,1:T(8,128)(2,1)}, u32[]{:S(2)}) copy-start(bf16[3072,96]{0,1:T(8,128)(2,1)} %param.18) | copy-start | bytes 1769476
  79.0 3.7 %copy-start.7 = (bf16[4,96]{1,0:T(4,128)(2,1)S(1)}, bf16[4,96]{1,0:T(4,128)(2,1)}, u32[]{:S(2)}) copy-start(bf16[4,96]{1,0:T(4,128)(2,1)} %residual_ref.1) | copy-start | bytes 2308
  79.7 18.6 %copy-start = (bf16[2,6144,128]{2,1,0:T(8,128)(2,1)S(1)}, bf16[2,6144,128]{2,1,0:T(8,128)(2,1)}, u32[]{:S(2)}) copy-start(bf16[2,6144,128]{2,1,0:T(8,128)(2,1)} %gate_ref.1) | copy-start | bytes 9437188
  79.7 18.6 %copy-start.1 = (bf16[2,6144,128]{2,1,0:T(8,128)(2,1)S(1)}, bf16[2,6144,128]{2,1,0:T(8,128)(2,1)}, u32[]{:S(2)}) copy-start(bf16[2,6144,128]{2,1,0:T(8,128)(2,1)} %up_ref.1) | copy-start | bytes 9437188
  79.7 18.6 %copy-start.2 = (bf16[2,128,6144]{2,1,0:T(8,128)(2,1)S(1)}, bf16[2,128,6144]{2,1,0:T(8,128)(2,1)}, u32[]{:S(2)}) copy-start(bf16[2,128,6144]{2,1,0:T(8,128)(2,1)} %down_ref.1) | copy-start | bytes 9437188
  79.7 18.6 %copy-start.3 = (bf16[6144,4]{0,1:T(4,128)(2,1)S(1)}, bf16[6144,4]{0,1:T(4,128)(2,1)}, u32[]{:S(2)}) copy-start(bf16[6144,4]{0,1:T(4,128)(2,1)} %param.20) | copy-start | bytes 147460
  79.8 18.5 %copy-start.4 = (bf16[6144]{0:T(1024)(128)(2,1)S(1)}, bf16[6144]{0:T(1024)(128)(2,1)}, u32[]{:S(2)}) copy-start(bf16[6144]{0:T(1024)(128)(2,1)} %gain_ref.1) | copy-start | bytes 36868
  79.8 18.5 %copy-start.5 = (s32[4,2]{0,1:T(2,128)S(1)}, s32[4,2]{0,1:T(2,128)}, u32[]{:S(2)}) copy-start(s32[4,2]{0,1:T(2,128)} %param.17) | copy-start | bytes 100
  79.8 2.9 %collective-permute-start.2 = (f32[4,96]{1,0:T(4,128)S(1)}, f32[4,96]{1,0:T(4,128)S(1)}, u32[]{:S(2)}, u32[]{:S(2)}) collective-permute-start(f32[4,96]{1,0:T(4,128)S(1)} %project.1.left_ref), channel_id=1, source_target_pairs={{0,1},{1,0},{2,3},{3,2},{4,5},{5,4},{6,7},{7,6},{8,9},{9,8},{10,11... | collective-permute-start | bytes 4616 | tf_op jit(solution)/shard_map/ppermute | solution.py:55
  116.5 3.9 %collective-permute-start.3 = (f32[4,96]{1,0:T(4,128)S(1)}, f32[4,96]{1,0:T(4,128)S(1)}, u32[]{:S(2)}, u32[]{:S(2)}) collective-permute-start(f32[4,96]{1,0:T(4,128)S(1)} %reduce_sum.9), channel_id=1, source_target_pairs={{0,1},{1,0},{2,3},{3,2},{4,5},{5,4},{6,7},{7,6},{8,9},{9,8},{10,11... | collective-permute-start | bytes 4616 | tf_op jit(solution)/shard_map/ppermute | solution.py:55

commit v5 on v2

--- a/solution.py
+++ b/solution.py
@@ -25,6 +25,7 @@
 LOW = -1e30
 LARGEST = 6.0
 SCALE = 1.0 / math.sqrt(HD)
+AFTER_TRANSFER = pl.CostEstimate(flops=20_000_000_000, transcendentals=0, bytes_accessed=1 << 24)
 PARAMS = pltpu.CompilerParams(vmem_limit_bytes=16 << 20)
 NT = (((1,), (1,)), ((), ()))
 NN = (((1,), (0,)), ((), ()))
@@ -228,6 +229,7 @@
         out_specs=vmem(),
         out_shape=pltpu.VMEM((peers, tiles, ROWS, LANES), BF16),
         compiler_params=PARAMS,
+        cost_estimate=AFTER_TRANSFER,
         name="weights",
     )(near(parts), near(limit))
 
@@ -282,6 +284,7 @@
         out_specs=vmem(),
         out_shape=pltpu.VMEM((depth + ROWS, LANES), F32),
         compiler_params=PARAMS,
+        cost_estimate=AFTER_TRANSFER,
         name="values",
     )(near(weights), near(kv_cache))
 
@@ -313,6 +316,7 @@
         out_specs=vmem(),
         out_shape=pltpu.VMEM((copies, ROWS, LANES), BF16),
         compiler_params=PARAMS,
+        cost_estimate=AFTER_TRANSFER,
         name="merge",
     )(near(own), near(left), near(right))
 
@@ -364,6 +368,7 @@
         out_specs=vmem(),
         out_shape=pltpu.VMEM((requests, w_out.shape[1]), F32),
         compiler_params=PARAMS,
+        cost_estimate=AFTER_TRANSFER,
         name="project",
     )(near(attn), near(w_out.T))
 
@@ -385,13 +390,12 @@
             pltpu.VMEM((copies, *residual.shape), BF16),
         ],
         compiler_params=PARAMS,
+        cost_estimate=AFTER_TRANSFER,
         name="attend",
     )(near(residual), near(left), near(right))
 
 
-def expert_kernel(x_ref, gain_ref, router_ref, routing_ref, gate_ref, up_ref, far_ref, out_ref, down_ref, sem):
-    fetch = pltpu.make_async_copy(far_ref, down_ref, sem)
-    fetch.start()
+def expert_kernel(x_ref, gain_ref, router_ref, routing_ref, gate_ref, up_ref, down_ref, out_ref):
     requests = x_ref.shape[1]
     model = gain_ref.shape[0]
     held, _, hidden = gate_ref.shape
@@ -424,7 +428,6 @@
         up = lax.dot_general(normed, up_ref[k], NN, preferred_element_type=F32)
         active.append((jax.nn.silu(gate) * up * share).astype(BF16))
     activation = jnp.concatenate(active, axis=-1)
-    fetch.wait()
     down = down_ref[...].reshape(held * hidden, model)
     terms = lax.dot_general(activation, down, NN, preferred_element_type=F32)
     for k in range(blocks):
@@ -436,14 +439,8 @@
     model = norm_gain.shape[0]
     return pl.pallas_call(
         expert_kernel,
-        in_specs=[
-            *[vmem()] * 3,
-            pl.BlockSpec(memory_space=pltpu.SMEM),
-            *[vmem()] * 2,
-            pl.BlockSpec(memory_space=pltpu.HBM),
-        ],
+        in_specs=[vmem()] * 3 + [pl.BlockSpec(memory_space=pltpu.SMEM)] + [vmem()] * 3,
         out_specs=vmem(),
-        scratch_shapes=[pltpu.VMEM(w_down.shape, BF16), pltpu.SemaphoreType.DMA],
         out_shape=pltpu.VMEM((seq_count, requests, model // seq_count), F32),
         compiler_params=PARAMS,
         name="experts",
@@ -454,7 +451,7 @@
         routing.T,
         near(w_gate),
         near(w_up),
-        far(w_down),
+        near(w_down),
     )
 
 

time: 122 us -> 121 us (level)
  Pallas kernels: 9.08 us -> 7.24 us
    pallas_call x1, Pallas kernels: 4.11 us -> 2.27 us  [experts(): pl.pallas_call(expert_kernel, in_specs=[vmem()] * 3 + [pl.BlockSpec(memor...]
where the time goes in v5:
time: 121 us; the launch traced here: 120 us
  blocking collectives  82.2 us (68%)
  starting transfers between devices  27 us (22%)
  Pallas kernels  7.24 us (6%)
  waiting for transfers between devices  1.92 us (2%)
    all_to_all x5, blocking collectives, to_everyone(): return lax.all_to_all(copies, axes, split_axis=0, concat_axis=0, tiled=True)  82.2 us
    ppermute x4, starting transfers between devices, swapped(): return lax.ppermute(shard, E, [(0, 1), (1, 0)])  27 us
  transfers between devices with their start and end apart: 4, of which 3 were waited for; matrix products, arithmetic and copies ran while one was open for 0% of the time, Pallas kernels for 1%

profile of v5, /device:TPU:513, one launch (start us, length us, event | category | flops | bytes accessed | tf_op | source)
XLA Modules:
  0.0 120.4 jit_solution(12871487842469985986)
XLA Ops:
  0.6 0.8 pack.1
  1.4 20.5 %collective-permute-start = (bf16[4,1024]{1,0:T(4,128)(2,1)S(1)}, bf16[4,1024]{1,0:T(4,128)(2,1)S(1)}, u32[]{:S(2)}, u32[]{:S(2)}) collective-permute-start(bf16[4,1024]{1,0:T(4,128)(2,1)S(1)} %get-tuple-element.8.refs_0_), channel_id=1, source_target_pairs={{0,1},{1,0},{2,3},{3,2},{4,5},{5,4},{6,7},{7,6},{8,9},{9,8},{10,11... | collective-permute-start | bytes 24584 | tf_op jit(solution)/shard_map/ppermute | solution.py:55
  21.9 1.2 %keys.1.refs_2_ = bf16[16,32768]{1,0:T(8,128)(2,1)S(1)} custom-call(bf16[2,16,32768]{2,1,0:T(8,128)(2,1)} %refs_1_.1), custom_call_target="tpu_custom_call" | custom-call | tf_op jit(solution)/shard_map/keys/pallas_call | solution.py:156
  23.2 0.0 collective-permute-done.refs_1_
  23.2 0.9 scores.1
  24.1 17.6 %all_to_all.25.refs_0_ = bf16[8,24,1024]{2,1,0:T(8,128)(2,1)S(1)} all-to-all(bf16[8,24,1024]{2,1,0:T(8,128)(2,1)S(1)} %get-tuple-element.10), channel_id=1, replica_groups=mesh['groups'=2,'seq_0'=8,'seq_1'=8,'expert'=2] {'seq_1'}, dimensions={0} | all-to-all | bytes 786432 | tf_op jit(solution)/shard_map/all_to_all | solution.py:59
  41.6 0.0 copy-start.3
  41.7 0.5 weights.1
  42.2 17.3 %all_to_all.26.refs_0_ = bf16[8,25,8,128]{3,2,1,0:T(8,128)(2,1)S(1)} all-to-all(bf16[8,25,8,128]{3,2,1,0:T(8,128)(2,1)S(1)} %weights.1), channel_id=1, replica_groups=mesh['groups'=2,'seq_0'=8,'seq_1'=8,'expert'=2] {'seq_1'}, dimensions={0} | all-to-all | bytes 819200 | tf_op jit(solution)/shard_map/all_to_all | solution.py:59
  59.4 0.0 copy-done.3
  59.4 0.7 values.1.left_ref
  60.2 1.4 %collective-permute-start.1 = (f32[24,128]{1,0:T(8,128)S(1)}, f32[24,128]{1,0:T(8,128)S(1)}, u32[]{:S(2)}, u32[]{:S(2)}) collective-permute-start(f32[24,128]{1,0:T(8,128)S(1)} %values.1.left_ref), channel_id=1, source_target_pairs={{0,1},{1,0},{2,3},{3,2},{4,5},{5,4},{6,7},{7,6},{8,9},{9,8},{10,11... | collective-permute-start | bytes 36872 | tf_op jit(solution)/shard_map/ppermute | solution.py:55
  61.6 0.8 collective-permute-done.1.right_ref
  62.4 0.0 copy-start.7
  62.4 0.1 merge.1
  62.5 16.0 %all_to_all.27.refs_0_ = bf16[64,8,128]{2,1,0:T(8,128)(2,1)S(1)} all-to-all(bf16[64,8,128]{2,1,0:T(8,128)(2,1)S(1)} %merge.1), channel_id=1, replica_groups=mesh['groups'=2,'seq_0'=8,'seq_1'=8,'expert'=2] {'seq_0','seq_1'}, dimensions={0} | all-to-all | bytes 262144 | tf_op jit(solution)/shard_map/all_to_all | solution.py:59
  78.5 0.0 copy-done.7
  78.5 0.0 copy-start.8
  78.5 0.7 project.1.left_ref
  79.2 0.0 copy-start
  79.2 0.0 copy-start.1
  79.2 0.0 copy-start.2
  79.2 0.1 copy-start.4
  79.3 0.0 copy-start.5
  79.3 0.0 copy-start.6
  79.4 2.1 %collective-permute-start.2 = (f32[4,96]{1,0:T(4,128)S(1)}, f32[4,96]{1,0:T(4,128)S(1)}, u32[]{:S(2)}, u32[]{:S(2)}) collective-permute-start(f32[4,96]{1,0:T(4,128)S(1)} %project.1.left_ref), channel_id=1, source_target_pairs={{0,1},{1,0},{2,3},{3,2},{4,5},{5,4},{6,7},{7,6},{8,9},{9,8},{10,11... | collective-permute-start | bytes 4616 | tf_op jit(solution)/shard_map/ppermute | solution.py:55
  81.4 0.8 collective-permute-done.2.right_ref
  82.2 0.0 copy-done.8
  82.3 15.5 %all_to_all.28.x_ref = bf16[64,4,96]{2,1,0:T(4,128)(2,1)S(1)} all-to-all(bf16[64,4,96]{2,1,0:T(4,128)(2,1)S(1)} %get-tuple-element.13), channel_id=1, replica_groups=mesh['groups'=2,'seq_0'=8,'seq_1'=8,'expert'=2] {'seq_0','seq_1'}, dimensions={0} | all-to-all | bytes 98304 | tf_op jit(solution)/shard_map/all_to_all | solution.py:59
  97.8 0.0 copy-done
  97.8 0.0 copy-done.1
  97.8 0.0 copy-done.2
  97.8 0.0 copy-done.4
  97.8 0.0 copy-done.5
  97.8 0.0 copy-done.6
  97.9 2.3 %experts.1 = f32[64,4,96]{2,1,0:T(4,128)S(1)} custom-call(bf16[64,4,96]{2,1,0:T(4,128)(2,1)S(1)} %all_to_all.28.x_ref, bf16[6144]{0:T(1024)(128)(2,1)S(1)} %copy-done.5, bf16[4,6144]{1,0:T(4,128)(2,1)S(1)} %bitcast.3, s32[2,4]{1,0:T(2,128)S(1)} %bitcast.4, bf16[2,6144,128]{2,1,0:T(8,128)(2,1)S(1)} %copy-done, bf16[2,6144,128]{2,1,0:T(8,128)(2,1)S(1)} %copy-done.1, ...), custom_call_target="tpu_custom_call" | custom-call | tf_op jit(solution)/shard_map/experts/pallas_call | solution.py:440
  100.1 15.8 %all_to_all.29 = f32[64,4,96]{2,1,0:T(4,128)S(1)} all-to-all(f32[64,4,96]{2,1,0:T(4,128)S(1)} %experts.1), channel_id=1, replica_groups=mesh['groups'=2,'seq_0'=8,'seq_1'=8,'expert'=2] {'seq_0','seq_1'}, dimensions={0} | all-to-all | bytes 196608 | tf_op jit(solution)/shard_map/all_to_all | solution.py:59
  115.9 0.1 reduce_sum.9
  116.0 3.0 %collective-permute-start.3 = (f32[4,96]{1,0:T(4,128)S(1)}, f32[4,96]{1,0:T(4,128)S(1)}, u32[]{:S(2)}, u32[]{:S(2)}) collective-permute-start(f32[4,96]{1,0:T(4,128)S(1)} %reduce_sum.9), channel_id=1, source_target_pairs={{0,1},{1,0},{2,3},{3,2},{4,5},{5,4},{6,7},{7,6},{8,9},{9,8},{10,11... | collective-permute-start | bytes 4616 | tf_op jit(solution)/shard_map/ppermute | solution.py:55
  119.1 0.6 copy.14
  119.6 0.3 collective-permute-done.3
  119.9 0.6 add_convert_fusion
  (1 shorter events, 0.0 us)
Async XLA Ops:
  1.4 21.8 %collective-permute-start = (bf16[4,1024]{1,0:T(4,128)(2,1)S(1)}, bf16[4,1024]{1,0:T(4,128)(2,1)S(1)}, u32[]{:S(2)}, u32[]{:S(2)}) collective-permute-start(bf16[4,1024]{1,0:T(4,128)(2,1)S(1)} %get-tuple-element.8.refs_0_), channel_id=1, source_target_pairs={{0,1},{1,0},{2,3},{3,2},{4,5},{5,4},{6,7},{7,6},{8,9},{9,8},{10,11... | collective-permute-start | bytes 24584 | tf_op jit(solution)/shard_map/ppermute | solution.py:55
  41.6 17.8 %copy-start.3 = (bf16[2,16,32768]{2,1,0:T(8,128)(2,1)S(1)}, bf16[2,16,32768]{2,1,0:T(8,128)(2,1)}, u32[]{:S(2)}) copy-start(bf16[2,16,32768]{2,1,0:T(8,128)(2,1)} %refs_1_.1) | copy-start | bytes 6291460
  60.2 2.3 %collective-permute-start.1 = (f32[24,128]{1,0:T(8,128)S(1)}, f32[24,128]{1,0:T(8,128)S(1)}, u32[]{:S(2)}, u32[]{:S(2)}) collective-permute-start(f32[24,128]{1,0:T(8,128)S(1)} %values.1.left_ref), channel_id=1, source_target_pairs={{0,1},{1,0},{2,3},{3,2},{4,5},{5,4},{6,7},{7,6},{8,9},{9,8},{10,11... | collective-permute-start | bytes 36872 | tf_op jit(solution)/shard_map/ppermute | solution.py:55
  62.4 16.1 %copy-start.7 = (bf16[3072,96]{0,1:T(8,128)(2,1)S(1)}, bf16[3072,96]{0,1:T(8,128)(2,1)}, u32[]{:S(2)}) copy-start(bf16[3072,96]{0,1:T(8,128)(2,1)} %param.18) | copy-start | bytes 1769476
  78.5 3.7 %copy-start.8 = (bf16[4,96]{1,0:T(4,128)(2,1)S(1)}, bf16[4,96]{1,0:T(4,128)(2,1)}, u32[]{:S(2)}) copy-start(bf16[4,96]{1,0:T(4,128)(2,1)} %residual_ref.1) | copy-start | bytes 2308
  79.2 18.6 %copy-start = (bf16[2,6144,128]{2,1,0:T(8,128)(2,1)S(1)}, bf16[2,6144,128]{2,1,0:T(8,128)(2,1)}, u32[]{:S(2)}) copy-start(bf16[2,6144,128]{2,1,0:T(8,128)(2,1)} %gate_ref.1) | copy-start | bytes 9437188
  79.2 18.6 %copy-start.1 = (bf16[2,6144,128]{2,1,0:T(8,128)(2,1)S(1)}, bf16[2,6144,128]{2,1,0:T(8,128)(2,1)}, u32[]{:S(2)}) copy-start(bf16[2,6144,128]{2,1,0:T(8,128)(2,1)} %up_ref.1) | copy-start | bytes 9437188
  79.2 18.6 %copy-start.2 = (bf16[2,128,6144]{2,1,0:T(8,128)(2,1)S(1)}, bf16[2,128,6144]{2,1,0:T(8,128)(2,1)}, u32[]{:S(2)}) copy-start(bf16[2,128,6144]{2,1,0:T(8,128)(2,1)} %down_ref.1) | copy-start | bytes 9437188
  79.2 18.6 %copy-start.4 = (bf16[6144,4]{0,1:T(4,128)(2,1)S(1)}, bf16[6144,4]{0,1:T(4,128)(2,1)}, u32[]{:S(2)}) copy-start(bf16[6144,4]{0,1:T(4,128)(2,1)} %param.20) | copy-start | bytes 147460
  79.3 18.5 %copy-start.5 = (bf16[6144]{0:T(1024)(128)(2,1)S(1)}, bf16[6144]{0:T(1024)(128)(2,1)}, u32[]{:S(2)}) copy-start(bf16[6144]{0:T(1024)(128)(2,1)} %gain_ref.1) | copy-start | bytes 36868
  79.3 18.5 %copy-start.6 = (s32[4,2]{0,1:T(2,128)S(1)}, s32[4,2]{0,1:T(2,128)}, u32[]{:S(2)}) copy-start(s32[4,2]{0,1:T(2,128)} %param.17) | copy-start | bytes 100
  79.4 2.9 %collective-permute-start.2 = (f32[4,96]{1,0:T(4,128)S(1)}, f32[4,96]{1,0:T(4,128)S(1)}, u32[]{:S(2)}, u32[]{:S(2)}) collective-permute-start(f32[4,96]{1,0:T(4,128)S(1)} %project.1.left_ref), channel_id=1, source_target_pairs={{0,1},{1,0},{2,3},{3,2},{4,5},{5,4},{6,7},{7,6},{8,9},{9,8},{10,11... | collective-permute-start | bytes 4616 | tf_op jit(solution)/shard_map/ppermute | solution.py:55
  116.0 3.9 %collective-permute-start.3 = (f32[4,96]{1,0:T(4,128)S(1)}, f32[4,96]{1,0:T(4,128)S(1)}, u32[]{:S(2)}, u32[]{:S(2)}) collective-permute-start(f32[4,96]{1,0:T(4,128)S(1)} %reduce_sum.9), channel_id=1, source_target_pairs={{0,1},{1,0},{2,3},{3,2},{4,5},{5,4},{6,7},{7,6},{8,9},{9,8},{10,11... | collective-permute-start | bytes 4616 | tf_op jit(solution)/shard_map/ppermute | solution.py:55

commit v6 on v5

--- a/solution.py
+++ b/solution.py
@@ -368,7 +368,6 @@
         out_specs=vmem(),
         out_shape=pltpu.VMEM((requests, w_out.shape[1]), F32),
         compiler_params=PARAMS,
-        cost_estimate=AFTER_TRANSFER,
         name="project",
     )(near(attn), near(w_out.T))
 
@@ -390,7 +389,6 @@
             pltpu.VMEM((copies, *residual.shape), BF16),
         ],
         compiler_params=PARAMS,
-        cost_estimate=AFTER_TRANSFER,
         name="attend",
     )(near(residual), near(left), near(right))
 

time: 121 us -> 121 us (level)
  no operation moved by 1% of the time
where the time goes in v6:
time: 121 us; the launch traced here: 120 us
  blocking collectives  82.6 us (68%)
  starting transfers between devices  26.7 us (22%)
  Pallas kernels  7.24 us (6%)
  waiting for transfers between devices  1.92 us (2%)
    all_to_all x5, blocking collectives, to_everyone(): return lax.all_to_all(copies, axes, split_axis=0, concat_axis=0, tiled=True)  82.6 us
    ppermute x4, starting transfers between devices, swapped(): return lax.ppermute(shard, E, [(0, 1), (1, 0)])  26.7 us
  transfers between devices with their start and end apart: 4, of which 3 were waited for; matrix products, arithmetic and copies ran while one was open for 0% of the time, Pallas kernels for 1%

profile of v6, /device:TPU:513, one launch (start us, length us, event | category | flops | bytes accessed | tf_op | source)
XLA Modules:
  0.0 120.5 jit_solution(14058365383405788554)
XLA Ops:
  0.6 0.8 pack.1
  1.4 20.5 %collective-permute-start = (bf16[4,1024]{1,0:T(4,128)(2,1)S(1)}, bf16[4,1024]{1,0:T(4,128)(2,1)S(1)}, u32[]{:S(2)}, u32[]{:S(2)}) collective-permute-start(bf16[4,1024]{1,0:T(4,128)(2,1)S(1)} %get-tuple-element.8.refs_0_), channel_id=1, source_target_pairs={{0,1},{1,0},{2,3},{3,2},{4,5},{5,4},{6,7},{7,6},{8,9},{9,8},{10,11... | collective-permute-start | bytes 24584 | tf_op jit(solution)/shard_map/ppermute | solution.py:55
  21.9 1.2 %keys.1.refs_2_ = bf16[16,32768]{1,0:T(8,128)(2,1)S(1)} custom-call(bf16[2,16,32768]{2,1,0:T(8,128)(2,1)} %refs_1_.1), custom_call_target="tpu_custom_call" | custom-call | tf_op jit(solution)/shard_map/keys/pallas_call | solution.py:156
  23.2 0.0 collective-permute-done.refs_1_
  23.2 0.9 scores.1
  24.1 17.6 %all_to_all.25.refs_0_ = bf16[8,24,1024]{2,1,0:T(8,128)(2,1)S(1)} all-to-all(bf16[8,24,1024]{2,1,0:T(8,128)(2,1)S(1)} %get-tuple-element.10), channel_id=1, replica_groups=mesh['groups'=2,'seq_0'=8,'seq_1'=8,'expert'=2] {'seq_1'}, dimensions={0} | all-to-all | bytes 786432 | tf_op jit(solution)/shard_map/all_to_all | solution.py:59
  41.6 0.0 copy-start.3
  41.7 0.5 weights.1
  42.2 17.3 %all_to_all.26.refs_0_ = bf16[8,25,8,128]{3,2,1,0:T(8,128)(2,1)S(1)} all-to-all(bf16[8,25,8,128]{3,2,1,0:T(8,128)(2,1)S(1)} %weights.1), channel_id=1, replica_groups=mesh['groups'=2,'seq_0'=8,'seq_1'=8,'expert'=2] {'seq_1'}, dimensions={0} | all-to-all | bytes 819200 | tf_op jit(solution)/shard_map/all_to_all | solution.py:59
  59.4 0.0 copy-done.3
  59.4 0.7 values.1.left_ref
  60.2 1.4 %collective-permute-start.1 = (f32[24,128]{1,0:T(8,128)S(1)}, f32[24,128]{1,0:T(8,128)S(1)}, u32[]{:S(2)}, u32[]{:S(2)}) collective-permute-start(f32[24,128]{1,0:T(8,128)S(1)} %values.1.left_ref), channel_id=1, source_target_pairs={{0,1},{1,0},{2,3},{3,2},{4,5},{5,4},{6,7},{7,6},{8,9},{9,8},{10,11... | collective-permute-start | bytes 36872 | tf_op jit(solution)/shard_map/ppermute | solution.py:55
  61.6 0.8 collective-permute-done.1.right_ref
  62.4 0.0 copy-start.4
  62.4 0.0 copy-start.7
  62.4 0.0 copy-start
  62.4 0.0 copy-start.1
  62.4 0.0 copy-start.2
  62.4 0.0 copy-start.5
  62.5 0.0 copy-start.6
  62.5 0.0 copy-start.8
  62.5 0.1 merge.1
  62.6 16.4 %all_to_all.27.refs_0_ = bf16[64,8,128]{2,1,0:T(8,128)(2,1)S(1)} all-to-all(bf16[64,8,128]{2,1,0:T(8,128)(2,1)S(1)} %merge.1), channel_id=1, replica_groups=mesh['groups'=2,'seq_0'=8,'seq_1'=8,'expert'=2] {'seq_0','seq_1'}, dimensions={0} | all-to-all | bytes 262144 | tf_op jit(solution)/shard_map/all_to_all | solution.py:59
  79.0 0.0 copy-done.4
  79.0 0.7 project.1.left_ref
  79.7 2.0 %collective-permute-start.2 = (f32[4,96]{1,0:T(4,128)S(1)}, f32[4,96]{1,0:T(4,128)S(1)}, u32[]{:S(2)}, u32[]{:S(2)}) collective-permute-start(f32[4,96]{1,0:T(4,128)S(1)} %project.1.left_ref), channel_id=1, source_target_pairs={{0,1},{1,0},{2,3},{3,2},{4,5},{5,4},{6,7},{7,6},{8,9},{9,8},{10,11... | collective-permute-start | bytes 4616 | tf_op jit(solution)/shard_map/ppermute | solution.py:55
  81.7 0.8 collective-permute-done.2.right_ref
  82.5 0.0 copy-done.7
  82.6 15.5 %all_to_all.28.x_ref = bf16[64,4,96]{2,1,0:T(4,128)(2,1)S(1)} all-to-all(bf16[64,4,96]{2,1,0:T(4,128)(2,1)S(1)} %get-tuple-element.13), channel_id=1, replica_groups=mesh['groups'=2,'seq_0'=8,'seq_1'=8,'expert'=2] {'seq_0','seq_1'}, dimensions={0} | all-to-all | bytes 98304 | tf_op jit(solution)/shard_map/all_to_all | solution.py:59
  98.1 0.0 copy-done
  98.1 0.0 copy-done.1
  98.1 0.0 copy-done.2
  98.1 0.0 copy-done.5
  98.1 0.0 copy-done.6
  98.1 0.0 copy-done.8
  98.1 2.3 %experts.1 = f32[64,4,96]{2,1,0:T(4,128)S(1)} custom-call(bf16[64,4,96]{2,1,0:T(4,128)(2,1)S(1)} %all_to_all.28.x_ref, bf16[6144]{0:T(1024)(128)(2,1)S(1)} %copy-done.6, bf16[4,6144]{1,0:T(4,128)(2,1)S(1)} %bitcast.4, s32[2,4]{1,0:T(2,128)S(1)} %bitcast.5, bf16[2,6144,128]{2,1,0:T(8,128)(2,1)S(1)} %copy-done, bf16[2,6144,128]{2,1,0:T(8,128)(2,1)S(1)} %copy-done.1, ...), custom_call_target="tpu_custom_call" | custom-call | tf_op jit(solution)/shard_map/experts/pallas_call | solution.py:438
  100.4 15.8 %all_to_all.29 = f32[64,4,96]{2,1,0:T(4,128)S(1)} all-to-all(f32[64,4,96]{2,1,0:T(4,128)S(1)} %experts.1), channel_id=1, replica_groups=mesh['groups'=2,'seq_0'=8,'seq_1'=8,'expert'=2] {'seq_0','seq_1'}, dimensions={0} | all-to-all | bytes 196608 | tf_op jit(solution)/shard_map/all_to_all | solution.py:59
  116.3 0.1 reduce_sum.9
  116.3 2.7 %collective-permute-start.3 = (f32[4,96]{1,0:T(4,128)S(1)}, f32[4,96]{1,0:T(4,128)S(1)}, u32[]{:S(2)}, u32[]{:S(2)}) collective-permute-start(f32[4,96]{1,0:T(4,128)S(1)} %reduce_sum.9), channel_id=1, source_target_pairs={{0,1},{1,0},{2,3},{3,2},{4,5},{5,4},{6,7},{7,6},{8,9},{9,8},{10,11... | collective-permute-start | bytes 4616 | tf_op jit(solution)/shard_map/ppermute | solution.py:55
  119.1 0.6 copy.14
  119.6 0.3 collective-permute-done.3
  119.9 0.6 add_convert_fusion
  (1 shorter events, 0.0 us)
Async XLA Ops:
  1.4 21.8 %collective-permute-start = (bf16[4,1024]{1,0:T(4,128)(2,1)S(1)}, bf16[4,1024]{1,0:T(4,128)(2,1)S(1)}, u32[]{:S(2)}, u32[]{:S(2)}) collective-permute-start(bf16[4,1024]{1,0:T(4,128)(2,1)S(1)} %get-tuple-element.8.refs_0_), channel_id=1, source_target_pairs={{0,1},{1,0},{2,3},{3,2},{4,5},{5,4},{6,7},{7,6},{8,9},{9,8},{10,11... | collective-permute-start | bytes 24584 | tf_op jit(solution)/shard_map/ppermute | solution.py:55
  41.6 17.8 %copy-start.3 = (bf16[2,16,32768]{2,1,0:T(8,128)(2,1)S(1)}, bf16[2,16,32768]{2,1,0:T(8,128)(2,1)}, u32[]{:S(2)}) copy-start(bf16[2,16,32768]{2,1,0:T(8,128)(2,1)} %refs_1_.1) | copy-start | bytes 6291460
  60.2 2.3 %collective-permute-start.1 = (f32[24,128]{1,0:T(8,128)S(1)}, f32[24,128]{1,0:T(8,128)S(1)}, u32[]{:S(2)}, u32[]{:S(2)}) collective-permute-start(f32[24,128]{1,0:T(8,128)S(1)} %values.1.left_ref), channel_id=1, source_target_pairs={{0,1},{1,0},{2,3},{3,2},{4,5},{5,4},{6,7},{7,6},{8,9},{9,8},{10,11... | collective-permute-start | bytes 36872 | tf_op jit(solution)/shard_map/ppermute | solution.py:55
  62.4 16.5 %copy-start.4 = (bf16[3072,96]{0,1:T(8,128)(2,1)S(1)}, bf16[3072,96]{0,1:T(8,128)(2,1)}, u32[]{:S(2)}) copy-start(bf16[3072,96]{0,1:T(8,128)(2,1)} %param.18) | copy-start | bytes 1769476
  62.4 20.1 %copy-start.7 = (bf16[4,96]{1,0:T(4,128)(2,1)S(1)}, bf16[4,96]{1,0:T(4,128)(2,1)}, u32[]{:S(2)}) copy-start(bf16[4,96]{1,0:T(4,128)(2,1)} %residual_ref.1) | copy-start | bytes 2308
  62.4 35.7 %copy-start = (bf16[2,6144,128]{2,1,0:T(8,128)(2,1)S(1)}, bf16[2,6144,128]{2,1,0:T(8,128)(2,1)}, u32[]{:S(2)}) copy-start(bf16[2,6144,128]{2,1,0:T(8,128)(2,1)} %gate_ref.1) | copy-start | bytes 9437188
  62.4 35.7 %copy-start.1 = (bf16[2,6144,128]{2,1,0:T(8,128)(2,1)S(1)}, bf16[2,6144,128]{2,1,0:T(8,128)(2,1)}, u32[]{:S(2)}) copy-start(bf16[2,6144,128]{2,1,0:T(8,128)(2,1)} %up_ref.1) | copy-start | bytes 9437188
  62.4 35.7 %copy-start.2 = (bf16[2,128,6144]{2,1,0:T(8,128)(2,1)S(1)}, bf16[2,128,6144]{2,1,0:T(8,128)(2,1)}, u32[]{:S(2)}) copy-start(bf16[2,128,6144]{2,1,0:T(8,128)(2,1)} %down_ref.1) | copy-start | bytes 9437188
  62.4 35.7 %copy-start.5 = (bf16[6144,4]{0,1:T(4,128)(2,1)S(1)}, bf16[6144,4]{0,1:T(4,128)(2,1)}, u32[]{:S(2)}) copy-start(bf16[6144,4]{0,1:T(4,128)(2,1)} %param.20) | copy-start | bytes 147460
  62.5 35.7 %copy-start.6 = (bf16[6144]{0:T(1024)(128)(2,1)S(1)}, bf16[6144]{0:T(1024)(128)(2,1)}, u32[]{:S(2)}) copy-start(bf16[6144]{0:T(1024)(128)(2,1)} %gain_ref.1) | copy-start | bytes 36868
  62.5 35.7 %copy-start.8 = (s32[4,2]{0,1:T(2,128)S(1)}, s32[4,2]{0,1:T(2,128)}, u32[]{:S(2)}) copy-start(s32[4,2]{0,1:T(2,128)} %param.17) | copy-start | bytes 100
  79.7 2.9 %collective-permute-start.2 = (f32[4,96]{1,0:T(4,128)S(1)}, f32[4,96]{1,0:T(4,128)S(1)}, u32[]{:S(2)}, u32[]{:S(2)}) collective-permute-start(f32[4,96]{1,0:T(4,128)S(1)} %project.1.left_ref), channel_id=1, source_target_pairs={{0,1},{1,0},{2,3},{3,2},{4,5},{5,4},{6,7},{7,6},{8,9},{9,8},{10,11... | collective-permute-start | bytes 4616 | tf_op jit(solution)/shard_map/ppermute | solution.py:55
  116.3 3.6 %collective-permute-start.3 = (f32[4,96]{1,0:T(4,128)S(1)}, f32[4,96]{1,0:T(4,128)S(1)}, u32[]{:S(2)}, u32[]{:S(2)}) collective-permute-start(f32[4,96]{1,0:T(4,128)S(1)} %reduce_sum.9), channel_id=1, source_target_pairs={{0,1},{1,0},{2,3},{3,2},{4,5},{5,4},{6,7},{7,6},{8,9},{9,8},{10,11... | collective-permute-start | bytes 4616 | tf_op jit(solution)/shard_map/ppermute | solution.py:55
